TPU v7x, 256 devices: a whole 4x4x8 slice. The times are simulated.
256 devices in a mesh: dom: 64 (over z, y, core), rep: 4 (over x).
Axes of the slice: x: 4, y: 4, z: 8, core: 2. Of those that a mesh axis runs over, the one named last changes fastest.
Arguments:
- ns_shape: bfloat16 [64, 256], replicated, may hold values from -0.75 to 0.75
- nm_shape: bfloat16 [64, 256], replicated, may hold values from -0.75 to 0.75
- sec_disp: bfloat16 [64, 2097152], P(None, ('dom', 'rep')), may hold values from -6 to 6
- mst_disp: bfloat16 [64, 2097152], P(None, ('dom', 'rep')), may hold values from -6 to 6
- gap_offset: float32 [2097152], P(('dom', 'rep')), may hold values from -6 to 6
- quad_weight: float32 [256], replicated, may hold values from 0.25 to 4
- jacobian: float32 [2097152], P(('dom', 'rep')), may hold values from 0.0005 to 0.005
- segment_slot: int32 [2097152], P(('dom', 'rep')), may hold values from 0 to 1279, as said below
- face_id: int32 [2097152], P(('dom', 'rep')), may hold values from 0 to 1073741823
- search_rank: int32 [2097152], P(('dom', 'rep')), may hold values from 0 to 3
- live_rows: int32 [256], P(('dom', 'rep')), may hold values from 1024 to 8192, as said below
Outputs:
- contact_force: bfloat16 [64, 2097152], P(None, ('dom', 'rep'))
- seg_pen: float32 [65536], P('dom')
- seg_face: int32 [65536], P('dom')
- seg_gap: float32 [65536], P('dom')
- mean_gap: float32 [], replicated
Inputs may be any that keep to these rules, and one draw needn't show every extreme that they name: `segment_slot`: A row's segment is (1024 times the dom index of its device plus its slot) modulo 65536; slots of 1024 or more reach the next dom index's first 256 segments. `live_rows`: entry b counts the live rows of the device with flat index b (dom-major); they are that device's first rows, the rest are padding; some device is full in every draw.
All inputs are finite; a program needn't handle non-finite values.
Results may differ from a plain program's by a relative error of at most 0.0055.
Values sent between devices are 32-bit elements; how exact they have to be, the bound alone decides.
A program may use at most 64 MiB of HBM per device.

v0:
```python
import math

import jax
import jax.numpy as jnp
from jax import lax
from jax.sharding import Mesh
from jax.sharding import PartitionSpec as P

SEG_DEV = 1024
SPILL = 256
DOM = ("dom_0", "dom_1", "dom_2")
DOM_REP = ("dom_0", "dom_1", "dom_2", "rep")


PENALTY = 400.0
LOWEST_FILL = -1e30
FACE_LIMIT = 1073741824


def passed_along(x, axis, by):
    length = lax.axis_size(axis)
    return lax.ppermute(x, axis, [(i, (i + by) % length) for i in range(length)])


def sent_to_all(x, axis):
    length = lax.axis_size(axis)
    return lax.all_to_all(jnp.broadcast_to(x[None], (length, *x.shape)), axis, 0, 0, tiled=True)


def all_in_one(x, axis):
    leaves = jax.tree.leaves(x)
    order = sorted(range(len(leaves)), key=lambda k: -leaves[k].size)
    width = (1, *leaves[order[0]].shape)[-1]
    lines = [
        jnp.pad(leaves[k].reshape(-1), (0, -leaves[k].size % width)).reshape(-1, width)
        for k in order
    ]
    both, at, found = (sent_to_all(jnp.concatenate(lines), axis), 0, {})
    for k, line in zip(order, lines):
        share = both[:, at : at + len(line)].reshape(len(both), -1)
        found[k] = share[:, : leaves[k].size].reshape(-1, *leaves[k].shape)
        at += len(line)
    numbers = iter(range(len(leaves)))
    return jax.tree.map(lambda _: found[next(numbers)], x)


def gathered_by_type(x, axis):
    leaves, found = (jax.tree.leaves(x), {})
    for first, a in enumerate(leaves):
        if first not in found:
            alike = [k for k, b in enumerate(leaves) if b.dtype == a.dtype]
            got = (
                all_in_one([leaves[k] for k in alike], axis)
                if len(alike) > 1
                else [sent_to_all(a, axis)]
            )
            for k, b in zip(alike, got):
                found[k] = b
    numbers = iter(range(len(leaves)))
    return jax.tree.map(lambda _: found[next(numbers)], x)


def combined_pairwise(pieces, combine):
    while len(jax.tree.leaves(pieces)[0]) > 1:
        pieces = jax.vmap(combine)(
            *(jax.tree.map(lambda part: part[side::2], pieces) for side in (0, 1))
        )
    return jax.tree.map(lambda part: part[0], pieces)


def joined_all(x, axis, combine):
    pieces = gathered_by_type(x, axis)
    return combined_pairwise(pieces, combine)


def over_axes(x, axes):
    for axis in axes:
        x = lax.psum(x, axis)
    return x


def project(shape_table, displace):
    return lax.dot_general(
        shape_table, displace, (((0,), (0,)), ((), ())), preferred_element_type=jnp.float32
    )


def combine(earlier, latter):
    prefer = (latter[1] > earlier[1]) | (latter[1] == earlier[1]) & (latter[2] < earlier[2])
    head = (
        jnp.maximum(earlier[0], latter[0]),
        jnp.where(prefer, latter[1], earlier[1]),
        jnp.where(prefer, latter[2], earlier[2]),
    )
    return head + tuple(
        (left_part + right_part for left_part, right_part in zip(earlier[3:], latter[3:]))
    )


def window_stats(gap_field, jac_row, weights, slots, faces, ranks, live, window_len):
    row_pen = jnp.max(-gap_field, axis=0)
    row_gap = jac_row * jnp.dot(weights, gap_field)
    row_area = jac_row * jnp.sum(weights)
    row_count = gap_field.shape[1]
    block_len = math.gcd(row_count, 1024)
    turns = row_count // block_len
    slot_ids = jnp.arange(window_len, dtype=jnp.int32)[:, None]
    paired = jnp.stack([row_gap, row_area], axis=0)

    def one_block(turn, carry):
        begin = turn * block_len

        def take(values):
            return lax.dynamic_slice_in_dim(values, begin, block_len, values.ndim - 1)

        block_live = take(live)
        block_ranks = take(ranks)
        member = slot_ids == take(slots)[None, :]
        hit = member & block_live[None, :]
        penalty_max = jnp.max(jnp.where(hit, take(row_pen)[None, :], LOWEST_FILL), axis=1)
        best_rank = jnp.max(jnp.where(hit, block_ranks[None, :], -1), axis=1)
        row_best = jnp.max(jnp.where(member, best_rank[:, None], -1), axis=0)
        chosen = jnp.where(block_live & (block_ranks == row_best), take(faces), FACE_LIMIT)
        lowest_face = jnp.min(jnp.where(member, chosen[None, :], FACE_LIMIT), axis=1)
        sums = lax.dot_general(take(paired), hit.astype(jnp.float32), (((1,), (1,)), ((), ())))
        fresh = (penalty_max, best_rank, lowest_face, sums[0], sums[1])
        return combine(carry, fresh)

    start = (
        jnp.full((window_len,), LOWEST_FILL, jnp.float32),
        jnp.full((window_len,), -1, jnp.int32),
        jnp.full((window_len,), FACE_LIMIT, jnp.int32),
        jnp.zeros((window_len,), jnp.float32),
        jnp.zeros((window_len,), jnp.float32),
    )
    return lax.fori_loop(0, turns, one_block, start)


def shards(
    ns_shape,
    nm_shape,
    sec_disp,
    mst_disp,
    gap_offset,
    quad_weight,
    jacobian,
    segment_slot,
    face_id,
    search_rank,
    live_rows,
):
    row_count = sec_disp.shape[1]
    window_len = SEG_DEV + SPILL
    gap_field = project(ns_shape, sec_disp) - project(nm_shape, mst_disp) + gap_offset[None, :]
    live = jnp.arange(row_count, dtype=jnp.int32) < live_rows[0]
    load = jnp.where(
        live[None, :],
        quad_weight[:, None] * jacobian[None, :] * PENALTY * jnp.maximum(-gap_field, 0.0),
        0.0,
    ).astype(jnp.bfloat16)
    contact_force = jnp.dot(ns_shape, load, preferred_element_type=jnp.float32).astype(jnp.bfloat16)
    stats = window_stats(
        gap_field, jacobian, quad_weight, segment_slot, face_id, search_rank, live, window_len
    )
    outgoing = tuple((part[SEG_DEV:] for part in stats))
    incoming = passed_along(outgoing, DOM, 1)
    leading = combine(tuple((part[:SPILL] for part in stats)), incoming)
    owned = tuple(
        (
            jnp.concatenate([lead_part, part[SPILL:SEG_DEV]])
            for lead_part, part in zip(leading, stats)
        )
    )
    own = joined_all(owned, "rep", combine)
    seg_pen = jnp.where(own[1] < 0, jnp.float32(0.0), own[0])
    seg_face = jnp.where(own[1] < 0, -1, own[2]).astype(jnp.int32)
    seg_gap = own[3]
    gap_total, area_total = (over_axes(jnp.sum(own[3]), DOM), over_axes(jnp.sum(own[4]), DOM))
    mean_gap = gap_total / area_total
    return (contact_force, seg_pen, seg_face, seg_gap, mean_gap)


def solution(mesh):
    finer = Mesh(
        mesh.devices.reshape(8, 4, 2, mesh.shape["rep"]), ("dom_0", "dom_1", "dom_2", "rep")
    )
    placed = (
        P(),
        P(),
        P(None, DOM_REP),
        P(None, DOM_REP),
        P(DOM_REP),
        P(),
        P(DOM_REP),
        P(DOM_REP),
        P(DOM_REP),
        P(DOM_REP),
        P(DOM_REP),
    )
    return jax.shard_map(
        shards,
        mesh=finer,
        in_specs=placed,
        out_specs=(P(None, DOM_REP), P(DOM), P(DOM), P(DOM), P()),
        check_vma=False,
    )
```

profile of v0, /device:TPU:1, one launch (start us, length us, event | category | flops | bytes accessed | tf_op | source)
XLA Modules:
  0.0 144.7 jit_solution(17707370756357591395)
XLA Ops:
  1.5 5.7 %fusion.31 = f32[256,8192]{1,0:T(8,128)} fusion(bf16[64,256]{1,0:T(8,128)(2,1)} %param.13, bf16[64,8192]{1,0:T(8,128)(2,1)} %param.15), kind=kOutput, calls=%fused_computation.70 | convolution fusion | flops 268435456 | bytes 9469952 | tf_op jit(solution)/shard_map/dot_general | solution.py:83
  7.8 4.8 %negate_reduce_fusion = (f32[8192]{0:T(1024)S(1)}, f32[256,8192]{1,0:T(8,128)S(1)}) fusion(f32[8192]{0:T(1024)S(1)} %copy-done.2, f32[256,8192]{1,0:T(8,128)} %fusion.31, bf16[64,256]{1,0:T(8,128)(2,1)S(1)} %copy-done.3, bf16[64,8192]{1,0:T(8,128)(2,1)S(1)} %copy-done), kind=kOutput, calls=%fused_computation.30 | convolution fusion | flops 276815872 | bytes 17924096 | tf_op jit(solution)/shard_map/dot_general | solution.py:83
  13.3 2.5 %copy-done.1 = f32[256,8192]{1,0:T(8,128)} copy-done((f32[256,8192]{1,0:T(8,128)}, f32[256,8192]{1,0:T(8,128)S(1)}, u32[]{:S(2)}) %copy-start.1) | copy-done | bytes 8388632
  16.6 58.6 %while.22 = (s32[]{:T(128)}, f32[1280]{0:T(1024)S(1)}, s32[1280]{0:T(1024)S(1)}, s32[1280]{0:T(1024)S(1)}, f32[1280]{0:T(1024)S(1)}, /*index=5*/f32[1280]{0:T(10...) while((s32[]{:T(128)}, f32[1280]{0:T(1024)S(1)}, ...), condition=%wide.region_7.8_spmd.clone, body=%wide.region_2.7_spmd.clone.sunk | while | flops 26231816 | bytes 216295 | solution.py:136
  19.2 1.3 fusion.51
  26.5 1.3 fusion.51
  33.9 1.3 fusion.51
  41.2 1.3 fusion.51
  48.5 1.3 fusion.51
  55.8 1.3 fusion.51
  63.1 1.3 fusion.51
  70.5 1.3 fusion.51
  75.2 2.8 %collective-permute-start.2 = (f32[256]{0:T(256)S(1)}, f32[256]{0:T(256)S(1)}, u32[]{:S(2)}, u32[]{:S(2)}) collective-permute-start(f32[256]{0:T(256)S(1)} %slice.161), channel_id=1, source_target_pairs={{0,4},{4,8},{8,12},{12,16},{16,20},{20,24},{24,28},{28,32},{32,36}... | collective-permute-start | bytes 3080 | tf_op jit(solution)/shard_map/ppermute | solution.py:22
  78.1 1.6 %collective-permute-start.4 = (f32[256]{0:T(256)S(1)}, f32[256]{0:T(256)S(1)}, u32[]{:S(2)}, u32[]{:S(2)}) collective-permute-start(f32[256]{0:T(256)S(1)} %slice.167), channel_id=1, source_target_pairs={{0,4},{4,8},{8,12},{12,16},{16,20},{20,24},{24,28},{28,32},{32,36}... | collective-permute-start | bytes 3080 | tf_op jit(solution)/shard_map/ppermute | solution.py:22
  79.8 1.3 collective-permute-start
  81.1 6.3 %fusion.20 = bf16[64,8192]{1,0:T(8,128)(2,1)} fusion(bf16[64,256]{1,0:T(8,128)(2,1)S(1)} %copy-done.4, f32[256,8192]{1,0:T(8,128)} %copy-done.1, f32[8192]{0:T(1024)S(1)} %copy-done.5, f32[256]{0:T(256)S(1)} %copy-done.6, pred[8192]{0:T(1024)(128)(4,1)S(1)} %get-tuple-element.461), kind=kOutput, calls=%fused_computation.28 | convolution fusion | flops 283639808 | bytes 9511936 | tf_op jit(solution)/shard_map/dot_general | solution.py:161
  88.1 4.0 %all-to-all-start = ((s32[4,2,1024]{2,1,0:T(2,128)}), s32[4,2,1024]{2,1,0:T(2,128)S(1)}, u32[]{:S(2)}, u32[]{:S(2)}) async-start(s32[4,2,1024]{2,1,0:T(2,128)} %broadcast_in_dim.160), calls=%async_computation | async-start | bytes 65536 | tf_op jit(solution)/shard_map/all_to_all | solution.py:27
  92.2 4.5 %all-to-all-done = s32[4,2,1024]{2,1,0:T(2,128)S(1)} async-done(((s32[4,2,1024]{2,1,0:T(2,128)}), s32[4,2,1024]{2,1,0:T(2,128)S(1)}, u32[]{:S(2)}, u32[]{:S(2)}) %all-to-all-start) | async-done | bytes 32800 | tf_op jit(solution)/shard_map/all_to_all | solution.py:27
  97.4 3.3 %all-to-all-start.1 = ((f32[4,3,1024]{2,1,0:T(4,128)}), f32[4,3,1024]{2,1,0:T(4,128)S(1)}, u32[]{:S(2)}, u32[]{:S(2)}) async-start(f32[4,3,1024]{2,1,0:T(4,128)} %broadcast_in_dim.162), calls=%async_computation.1 | async-start | bytes 131072 | tf_op jit(solution)/shard_map/all_to_all | solution.py:27
  101.5 3.6 %all-to-all-done.1 = f32[4,3,1024]{2,1,0:T(4,128)S(1)} async-done(((f32[4,3,1024]{2,1,0:T(4,128)}), f32[4,3,1024]{2,1,0:T(4,128)S(1)}, u32[]{:S(2)}, u32[]{:S(2)}) %all-to-all-start.1) | async-done | bytes 49184 | tf_op jit(solution)/shard_map/all_to_all | solution.py:27
  106.0 1.2 fusion.27
  107.2 17.1 %all-reduce = (f32[]{:T(128)}, f32[]{:T(128)}) all-reduce(f32[]{:T(128)} %get-tuple-element.301, f32[]{:T(128)} %fusion.22), channel_id=1, replica_groups=mesh['dom_0'=8,'dom_1'=4,'dom_2'=2,'rep'=4] {'dom_0'}, use_global_device_ids=true, to_apply=%region_9.10 | all-reduce | flops 2 | bytes 16 | tf_op jit(solution)/shard_map/psum | solution.py:78
  124.3 7.5 %all-reduce.1 = (f32[]{:T(128)}, f32[]{:T(128)}) all-reduce(f32[]{:T(128)} %get-tuple-element.295, f32[]{:T(128)} %get-tuple-element.296), channel_id=1, replica_groups=mesh['dom_0'=8,'dom_1'=4,'dom_2'=2,'rep'=4] {'dom_1'}, use_global_device_ids=true, to_apply=%region_10.11 | all-reduce | flops 2 | bytes 16 | tf_op jit(solution)/shard_map/psum | solution.py:78
  131.7 9.8 %all-reduce.2 = (f32[]{:T(128)}, f32[]{:T(128)}) all-reduce(f32[]{:T(128)} %get-tuple-element.297, f32[]{:T(128)} %get-tuple-element.298), channel_id=1, replica_groups=mesh['dom_0'=8,'dom_1'=4,'dom_2'=2,'rep'=4] {'dom_2'}, use_global_device_ids=true, to_apply=%region_11.12 | all-reduce | flops 2 | bytes 16 | tf_op jit(solution)/shard_map/psum | solution.py:78
  (180 shorter events, 53.6 us)
Async XLA Ops:
  0.6 7.2 %copy-start = (bf16[64,8192]{1,0:T(8,128)(2,1)S(1)}, bf16[64,8192]{1,0:T(8,128)(2,1)}, u32[]{:S(2)}) copy-start(bf16[64,8192]{1,0:T(8,128)(2,1)} %param.16) | copy-start | bytes 3145732
  0.6 6.6 %copy-start.6 = (f32[256]{0:T(256)S(1)}, f32[256]{0:T(256)}, u32[]{:S(2)}) copy-start(f32[256]{0:T(256)} %param.18) | copy-start | bytes 3076
  0.7 7.2 %copy-start.3 = (bf16[64,256]{1,0:T(8,128)(2,1)S(1)}, bf16[64,256]{1,0:T(8,128)(2,1)}, u32[]{:S(2)}) copy-start(bf16[64,256]{1,0:T(8,128)(2,1)} %param.14) | copy-start | bytes 98308
  0.7 7.2 %copy-start.2 = (f32[8192]{0:T(1024)S(1)}, f32[8192]{0:T(1024)}, u32[]{:S(2)}) copy-start(f32[8192]{0:T(1024)} %param.17) | copy-start | bytes 98308
  12.6 3.2 %copy-start.1 = (f32[256,8192]{1,0:T(8,128)}, f32[256,8192]{1,0:T(8,128)S(1)}, u32[]{:S(2)}) copy-start(f32[256,8192]{1,0:T(8,128)S(1)} %get-tuple-element.321) | copy-start | bytes 25165828
  12.7 3.2 %copy-start.5 = (f32[8192]{0:T(1024)S(1)}, f32[8192]{0:T(1024)}, u32[]{:S(2)}) copy-start(f32[8192]{0:T(1024)} %param.19) | copy-start | bytes 98308
  16.6 64.5 %copy-start.4 = (bf16[64,256]{1,0:T(8,128)(2,1)S(1)}, bf16[64,256]{1,0:T(8,128)(2,1)}, u32[]{:S(2)}) copy-start(bf16[64,256]{1,0:T(8,128)(2,1)} %param.13) | copy-start | bytes 98308
  75.2 16.9 %collective-permute-start.2 = (f32[256]{0:T(256)S(1)}, f32[256]{0:T(256)S(1)}, u32[]{:S(2)}, u32[]{:S(2)}) collective-permute-start(f32[256]{0:T(256)S(1)} %slice.161), channel_id=1, source_target_pairs={{0,4},{4,8},{8,12},{12,16},{16,20},{20,24},{24,28},{28,32},{32,36}... | collective-permute-start | bytes 3080 | tf_op jit(solution)/shard_map/ppermute | solution.py:22
  78.0 14.1 %collective-permute-start.3 = (f32[256]{0:T(256)S(1)}, f32[256]{0:T(256)S(1)}, u32[]{:S(2)}, u32[]{:S(2)}) collective-permute-start(f32[256]{0:T(256)S(1)} %slice.164), channel_id=1, source_target_pairs={{0,4},{4,8},{8,12},{12,16},{16,20},{20,24},{24,28},{28,32},{32,36}... | collective-permute-start | bytes 3080 | tf_op jit(solution)/shard_map/ppermute | solution.py:22
  78.1 14.1 %collective-permute-start.4 = (f32[256]{0:T(256)S(1)}, f32[256]{0:T(256)S(1)}, u32[]{:S(2)}, u32[]{:S(2)}) collective-permute-start(f32[256]{0:T(256)S(1)} %slice.167), channel_id=1, source_target_pairs={{0,4},{4,8},{8,12},{12,16},{16,20},{20,24},{24,28},{28,32},{32,36}... | collective-permute-start | bytes 3080 | tf_op jit(solution)/shard_map/ppermute | solution.py:22
  79.7 7.7 %collective-permute-start.1 = (s32[256]{0:T(256)S(1)}, s32[256]{0:T(256)S(1)}, u32[]{:S(2)}, u32[]{:S(2)}) collective-permute-start(s32[256]{0:T(256)S(1)} %slice.146), channel_id=1, source_target_pairs={{0,4},{4,8},{8,12},{12,16},{16,20},{20,24},{24,28},{28,32},{32,36}... | collective-permute-start | bytes 3080 | tf_op jit(solution)/shard_map/ppermute | solution.py:22
  79.8 7.6 %collective-permute-start = (s32[256]{0:T(256)S(1)}, s32[256]{0:T(256)S(1)}, u32[]{:S(2)}, u32[]{:S(2)}) collective-permute-start(s32[256]{0:T(256)S(1)} %slice.144), channel_id=1, source_target_pairs={{0,4},{4,8},{8,12},{12,16},{16,20},{20,24},{24,28},{28,32},{32,36}... | collective-permute-start | bytes 3080 | tf_op jit(solution)/shard_map/ppermute | solution.py:22
  88.1 8.7 %all-to-all-start = ((s32[4,2,1024]{2,1,0:T(2,128)}), s32[4,2,1024]{2,1,0:T(2,128)S(1)}, u32[]{:S(2)}, u32[]{:S(2)}) async-start(s32[4,2,1024]{2,1,0:T(2,128)} %broadcast_in_dim.160), calls=%async_computation | async-start | bytes 65536 | tf_op jit(solution)/shard_map/all_to_all | solution.py:27
  97.4 7.7 %all-to-all-start.1 = ((f32[4,3,1024]{2,1,0:T(4,128)}), f32[4,3,1024]{2,1,0:T(4,128)S(1)}, u32[]{:S(2)}, u32[]{:S(2)}) async-start(f32[4,3,1024]{2,1,0:T(4,128)} %broadcast_in_dim.162), calls=%async_computation.1 | async-start | bytes 131072 | tf_op jit(solution)/shard_map/all_to_all | solution.py:27
where the time goes:
time: 146 us; the launch traced here: 145 us
  other arithmetic  42 us (29%)
  blocking collectives  34.4 us (24%)
  matrix products  26.5 us (18%)
  local copies, waits for them, and re-layouts  15.7 us (11%)
  starting transfers between devices  13.1 us (9%)
  waiting for transfers between devices  8.19 us (6%)
  between operations  4.18 us (3%)
    psum x3, blocking collectives, over_axes(): x = lax.psum(x, axis)  34.4 us
    dynamic_slice x32, local copies, waits for them, and re-layouts, take(): return lax.dynamic_slice_in_dim(values, begin, block_len, values.ndim - 1)  11.2 us
    dot_general x2, matrix products, project(): lax.dot_general(shape_table, displace, (((0,), (0,)), ((), ())), preferre...  10.6 us
    reduce_max x8, other arithmetic, one_block(): best_rank = jnp.max(jnp.where(hit, block_ranks[None, :], -1), axis=1)  10.2 us
    dot_general x8, matrix products, one_block(): lax.dot_general(take(paired), hit.astype(jnp.float32), (((1,), (1,)), (()...  9.07 us
    reduce_max x8, other arithmetic, one_block(): jnp.max(jnp.where(hit, take(row_pen)[None, :], LOWEST_FILL), axis=1)  8.89 us
    all_to_all x2, waiting for transfers between devices, sent_to_all(): lax.all_to_all(jnp.broadcast_to(x[None], (length, *x.shape)), axis, 0, 0,...  8.18 us
    all_to_all x2, starting transfers between devices, sent_to_all(): lax.all_to_all(jnp.broadcast_to(x[None], (length, *x.shape)), axis, 0, 0,...  7.29 us
  transfers between devices with their start and end apart: 7, of which 2 were waited for; matrix products, arithmetic and copies ran while one was open for 5% of the time, Pallas kernels for 0%

commit v1 on v0

v1 whole, which is shorter than its diff:
```python
import jax
import jax.numpy as jnp
from jax import lax
from jax.experimental import pallas as pl
from jax.experimental.pallas import tpu as pltpu
from jax.sharding import Mesh
from jax.sharding import PartitionSpec as P

SEG_DEV = 1024
SPILL = 256
P_SIZE = 256
K = 64
LANES = 128
HIS = 10
DOM = ("dom_0", "dom_1", "dom_2")
DOM_REP = ("dom_0", "dom_1", "dom_2", "rep")
PENALTY = 400.0
LOWEST_FILL = -1e30
FACE_LIMIT = 1073741824
KEY_LOW = -2147483648
CHUNK = 1024
F32 = jnp.float32
BF16 = jnp.bfloat16


def pieces(x):
    high = x.astype(BF16)
    rest = x - high.astype(F32)
    mid = rest.astype(BF16)
    low = (rest - mid.astype(F32)).astype(BF16)
    return high.astype(F32), mid.astype(F32), low.astype(F32)


def fold_rows(x, op):
    while x.shape[0] > 8:
        half = x.shape[0] // 2
        x = op(x[:half], x[half:])
    for shift in (4, 2, 1):
        x = op(x, pltpu.roll(x, shift, 0))
    return x


def local_kernel(
    ns_ref, nm_ref, sec_hbm, mst_hbm, off_ref, qw_ref, jac_ref, slot_ref, face_ref, rank_ref, live_ref,
    force_hbm, pen_ref, rank_out, face_out, gap_ref, area_ref,
    sec_buf, mst_buf, force_buf, table, weight, pen_by, key_by, lo_ref, acc_pen, acc_key, in_sem, out_sem,
):
    rows = sec_hbm.shape[1]
    chunks = rows // CHUNK

    def load(c):
        part = pl.ds(c * CHUNK, CHUNK)
        return (
            pltpu.make_async_copy(sec_hbm.at[:, part], sec_buf.at[:, part], in_sem.at[0, c]),
            pltpu.make_async_copy(mst_hbm.at[:, part], mst_buf.at[:, part], in_sem.at[1, c]),
        )

    def save(c):
        part = pl.ds(c * CHUNK, CHUNK)
        return pltpu.make_async_copy(force_buf.at[:, part], force_hbm.at[:, part], out_sem.at[c])

    for c in range(chunks):
        for copy in load(c):
            copy.start()

    ns = ns_ref[...]
    both = jnp.concatenate([ns.astype(F32), -nm_ref[...].astype(F32)], axis=0).T
    column = jnp.broadcast_to(qw_ref[...], (LANES, P_SIZE)).T
    weight[...] = column * (-PENALTY)
    total_weight = jnp.sum(qw_ref[...], axis=1, keepdims=True)
    coefficient = jnp.sum(both * column, axis=0, keepdims=True)
    high, mid, low = pieces(coefficient)
    eight = lax.broadcasted_iota(jnp.int32, (8, LANES), 0)
    extra = jnp.where(eight == 0, high, jnp.where(eight == 1, mid, jnp.where(eight == 2, low, 0.0)))
    lane = lax.broadcasted_iota(jnp.int32, (P_SIZE + 16, LANES), 1)
    row = lax.broadcasted_iota(jnp.int32, (P_SIZE + 16, LANES), 0)
    table[:, :LANES] = jnp.concatenate([both, extra, jnp.zeros_like(extra)], axis=0).astype(BF16)
    table[:, LANES:] = jnp.where((lane < 3) & (row < P_SIZE), 1.0, 0.0).astype(BF16)

    live_count = live_ref[0]
    sums = jnp.zeros((48, LANES), F32)
    area = jnp.zeros((1, CHUNK), F32)
    for c in range(chunks):
        part = pl.ds(c * CHUNK, CHUNK)
        offset, jacobian = off_ref[:, part], jac_ref[:, part]
        slots = slot_ref[:, part]
        live = lax.broadcasted_iota(jnp.int32, (1, CHUNK), 1) < live_count - c * CHUNK
        for copy in load(c):
            copy.wait()
        o_high, o_mid, o_low = pieces(offset)
        sixteen = lax.broadcasted_iota(jnp.int32, (16, CHUNK), 0)
        tail = jnp.where(
            sixteen == 0, o_high, jnp.where(sixteen == 1, o_mid, jnp.where(sixteen == 2, o_low, 0.0))
        ).astype(BF16)
        data = jnp.concatenate([sec_buf[:, part], mst_buf[:, part], tail], axis=0)
        found = jnp.dot(table[:, :144], data, preferred_element_type=F32)
        gap = found[:P_SIZE]
        row_pen = -jnp.min(gap, axis=0, keepdims=True)
        row_gap = jacobian * (
            found[P_SIZE : P_SIZE + 1]
            + found[P_SIZE + 1 : P_SIZE + 2]
            + found[P_SIZE + 2 : P_SIZE + 3]
            + offset * total_weight
        )
        column_weight = jnp.tile(weight[...], (1, CHUNK // LANES))
        load_field = (jnp.maximum(column_weight * gap, 0.0) * jnp.where(live, jacobian, 0.0)).astype(BF16)
        force_buf[:, part] = jnp.dot(ns, load_field, preferred_element_type=F32).astype(BF16)
        save(c).start()

        area = area + jnp.where(live, jacobian, 0.0)
        hi = jnp.where(live, lax.shift_right_logical(slots, 7), 99)
        lo = slots & (LANES - 1)
        member = sixteen == hi
        key = (rank_ref[:, part] - 2) * FACE_LIMIT + (FACE_LIMIT - 1 - face_ref[:, part])
        pens = jnp.where(member, row_pen, LOWEST_FILL)
        keys = jnp.where(member, key, KEY_LOW)
        for j in range(CHUNK // LANES):
            at = slice(j * LANES, (j + 1) * LANES)
            pen_by[c * (CHUNK // LANES) + j] = pens[:, at]
            key_by[c * (CHUNK // LANES) + j] = keys[:, at]
            lo_ref[c * (CHUNK // LANES) + j] = jnp.broadcast_to(lo[:, at], (8, LANES))
        split = jnp.concatenate([jnp.where(member, piece, 0.0) for piece in pieces(row_gap)], axis=0)
        ids = lax.broadcasted_iota(jnp.int32, (LANES, CHUNK), 0)
        one_hot = jnp.where(ids == lo, 1.0, 0.0).astype(BF16)
        sums = sums + lax.dot_general(
            split.astype(BF16), one_hot, (((1,), (1,)), ((), ())), preferred_element_type=F32
        )
    gap_ref[...] = sums[:16] + sums[16:32] + sums[32:]
    area_ref[...] = jnp.broadcast_to(jnp.sum(area, axis=1, keepdims=True) * total_weight, (8, LANES))

    group = 2
    for g in range(LANES // (8 * group)):
        ids = [eight + 8 * (g * group + j) for j in range(group)]

        def step(i, carry):
            pens, keys = carry
            lo = lo_ref[i]
            masks = [lo == ids[j] for j in range(group)]
            new_pens, new_keys = [], []
            for h in range(HIS):
                pen = pen_by[i, pl.ds(h, 8, stride=0), :]
                key = key_by[i, pl.ds(h, 8, stride=0), :]
                for j in range(group):
                    k = h * group + j
                    new_pens.append(jnp.maximum(pens[k], jnp.where(masks[j], pen, LOWEST_FILL)))
                    new_keys.append(jnp.maximum(keys[k], jnp.where(masks[j], key, KEY_LOW)))
            return new_pens, new_keys

        start = (
            [jnp.full((8, LANES), LOWEST_FILL, F32)] * (HIS * group),
            [jnp.full((8, LANES), KEY_LOW, jnp.int32)] * (HIS * group),
        )
        pens, keys = lax.fori_loop(0, rows // LANES, step, start, unroll=2)
        for h in range(HIS):
            for j in range(group):
                at = pl.ds(8 * (g * group + j), 8)
                acc_pen[h, at, :] = pens[h * group + j]
                acc_key[h, at, :] = keys[h * group + j]

    for h in range(HIS):
        pen = fold_rows(acc_pen[h].T, jnp.maximum)[:1]
        key = fold_rows(acc_key[h].T, jnp.maximum)[:1]
        empty = pen <= 0.5 * LOWEST_FILL
        pen_ref[h : h + 1, :] = pen
        rank_out[h : h + 1, :] = jnp.where(empty, -1, lax.shift_right_arithmetic(key, 30) + 2)
        face_out[h : h + 1, :] = jnp.where(empty, FACE_LIMIT, FACE_LIMIT - 1 - (key & (FACE_LIMIT - 1)))
    for c in range(chunks):
        save(c).wait()


def local_part(ns, nm, sec, mst, off, qw, jac, slot, face, rank, live):
    rows = sec.shape[1]
    chunks = rows // CHUNK
    vmem = pl.BlockSpec(memory_space=pltpu.VMEM)
    hbm = pl.BlockSpec(memory_space=pl.ANY)
    smem = pl.BlockSpec(memory_space=pltpu.SMEM)
    line = lambda x: x.reshape(1, -1)
    return pl.pallas_call(
        local_kernel,
        out_shape=(
            jax.ShapeDtypeStruct((K, rows), BF16),
            jax.ShapeDtypeStruct((16, LANES), F32),
            jax.ShapeDtypeStruct((16, LANES), jnp.int32),
            jax.ShapeDtypeStruct((16, LANES), jnp.int32),
            jax.ShapeDtypeStruct((16, LANES), F32),
            jax.ShapeDtypeStruct((8, LANES), F32),
        ),
        in_specs=[vmem, vmem, hbm, hbm, vmem, vmem, vmem, vmem, vmem, vmem, smem],
        out_specs=(hbm, vmem, vmem, vmem, vmem, vmem),
        scratch_shapes=[
            pltpu.VMEM((K, rows), BF16),
            pltpu.VMEM((K, rows), BF16),
            pltpu.VMEM((K, rows), BF16),
            pltpu.VMEM((P_SIZE + 16, 2 * LANES), BF16),
            pltpu.VMEM((P_SIZE, LANES), F32),
            pltpu.VMEM((rows // LANES, 16, LANES), F32),
            pltpu.VMEM((rows // LANES, 16, LANES), jnp.int32),
            pltpu.VMEM((rows // LANES, 8, LANES), jnp.int32),
            pltpu.VMEM((HIS, LANES, LANES), F32),
            pltpu.VMEM((HIS, LANES, LANES), jnp.int32),
            pltpu.SemaphoreType.DMA((2, chunks)),
            pltpu.SemaphoreType.DMA((chunks,)),
        ],
        compiler_params=pltpu.CompilerParams(vmem_limit_bytes=48 << 20),
    )(ns, nm, sec, mst, line(off), line(qw), line(jac), line(slot), line(face), line(rank), live)


def combine(earlier, latter):
    prefer = (latter[1] > earlier[1]) | (latter[1] == earlier[1]) & (latter[2] < earlier[2])
    return (
        jnp.maximum(earlier[0], latter[0]),
        jnp.where(prefer, latter[1], earlier[1]),
        jnp.where(prefer, latter[2], earlier[2]),
        earlier[3] + latter[3],
    )


def shards(*args):
    force, pen, rank, face, gap, area = local_part(*args)
    stats = (pen[:HIS], rank[:HIS], face[:HIS], gap[:HIS])
    length = lax.axis_size(DOM)
    moved = [(i, (i + 1) % length) for i in range(length)]
    incoming = [lax.ppermute(part[8:], DOM, moved) for part in stats]
    leading = combine([part[:2] for part in stats], incoming)
    owned = [jnp.concatenate([a, b[2:8]]) for a, b in zip(leading, stats)]
    shared = [lax.all_gather(part, "rep") for part in owned]
    own = [part[0] for part in shared]
    for k in range(1, 4):
        own = combine(own, [part[k] for part in shared])
    empty = own[1] < 0
    seg_pen = jnp.where(empty, 0.0, own[0]).reshape(-1)
    seg_face = jnp.where(empty, -1, own[2]).reshape(-1)
    totals = lax.psum((jnp.sum(gap), area[0, 0]), DOM_REP)
    return force, seg_pen, seg_face, own[3].reshape(-1), totals[0] / totals[1]


def solution(mesh):
    finer = Mesh(mesh.devices.reshape(8, 4, 2, mesh.shape["rep"]), DOM_REP)
    placed = (P(), P(), P(None, DOM_REP), P(None, DOM_REP), P(DOM_REP), P()) + (P(DOM_REP),) * 5
    return jax.shard_map(
        shards,
        mesh=finer,
        in_specs=placed,
        out_specs=(P(None, DOM_REP), P(DOM), P(DOM), P(DOM), P()),
        check_vma=False,
    )
```

time: 146 us -> 163 us (1.12)
  the two profiles are of different devices: /device:TPU:1 before, /device:TPU:32 now
where the time goes in v1:
time: 163 us
  blocking collectives  127 us (78%)
  Pallas kernels  16.4 us (10%)
  local copies, waits for them, and re-layouts  8.96 us (5%)
  between operations  3.86 us (2%)
  starting transfers between devices  3.44 us (2%)
  other arithmetic  2.46 us (2%)
    psum x1, blocking collectives, shards(): totals = lax.psum((jnp.sum(gap), area[0, 0]), DOM_REP)  79.3 us
    all_gather x4, blocking collectives, shards(): shared = [lax.all_gather(part, 'rep') for part in owned]  48.1 us
    pallas_call x1, Pallas kernels, local_part(): pl.pallas_call(local_kernel, out_shape=(jax.ShapeDtypeStruct((K, rows), B...  16.4 us
    unnamed x20, local copies, waits for them, and re-layouts  8.42 us
    ppermute x4, starting transfers between devices, shards(): incoming = [lax.ppermute(part[8:], DOM, moved) for part in stats]  3.44 us
  transfers between devices with their start and end apart: 4, of which 0 were waited for; matrix products, arithmetic and copies ran while one was open for 1% of the time, Pallas kernels for 0%

profile of v1, /device:TPU:32, one launch (start us, length us, event | category | flops | bytes accessed | tf_op | source)
XLA Modules:
  0.0 162.5 jit_solution(5701866529246927490)
XLA Ops:
  1.3 0.7 copy-done.9
  2.0 1.2 copy-done
  3.2 1.2 copy-done.1
  4.4 0.8 copy-done.2
  5.2 0.8 copy-done.3
  5.9 0.8 copy-done.4
  6.7 0.8 copy-done.5
  7.4 0.8 copy-done.6
  8.2 0.8 copy-done.7
  9.0 0.8 copy-done.8
  9.7 16.4 %shard_map.146 = (bf16[64,8192]{1,0:T(8,128)(2,1)}, f32[16,128]{1,0:T(8,128)S(1)}, s32[16,128]{1,0:T(8,128)S(1)}, s32[16,128]{1,0:T(8,128)S(1)}, f32[16,128]{1,0:T(8,128)S(1)}, /*index=5*/f32[8,128]{1,0:T(8,128)S(1)}) custom-call(bf16[64,256]{1,0:T(8,128)(2,1)S(1)} %copy-done.2, bf16[64,256]{1,0:T(8,128)(2,1)S(1)} %copy-done.3, ...), custom_call_target="tpu_custom_call" | custom-call | tf_op jit(solution)/shard_map/pallas_call | solution.py:178
  26.2 1.7 %collective-permute-start.1 = (s32[2,128]{1,0:T(2,128)S(1)}, s32[2,128]{1,0:T(2,128)S(1)}, u32[]{:S(2)}, u32[]{:S(2)}) collective-permute-start(s32[2,128]{1,0:T(2,128)S(1)} %slice.105), channel_id=1, source_target_pairs={{0,4},{4,8},{8,12},{12,16},{16,20},{20,24},{24,28},{28,32},{32,36}... | collective-permute-start | bytes 3080 | tf_op jit(solution)/shard_map/ppermute | solution.py:223
  27.9 0.1 collective-permute-start.2
  28.0 1.6 collective-permute-start.3
  29.6 0.6 reduce_sum.9
  30.2 0.5 slice.131
  30.7 79.3 %all-reduce = (f32[]{:T(128)}, f32[]{:T(128)}) all-reduce(f32[]{:T(128)} %reduce_sum.9, f32[]{:T(128)} %bitcast.16), channel_id=1, replica_groups=mesh['dom_0'=8,'dom_1'=4,'dom_2'=2,'rep'=4] {'dom_0','dom_1','dom_2','rep'}, use_global_device_ids=true, to_apply=%region_1.2 | all-reduce | flops 2 | bytes 16 | tf_op jit(solution)/shard_map/psum | solution.py:233
  111.5 12.0 %all-gather = s32[32,128]{1,0:T(8,128)S(1)} all-gather(s32[8,128]{1,0:T(8,128)S(1)} %pad_add_fusion), channel_id=2, replica_groups=mesh['dom_0'=8,'dom_1'=4,'dom_2'=2,'rep'=4] {'rep'}, dimensions={0}, use_global_device_ids=true | all-gather | bytes 20480 | tf_op jit(solution)/shard_map/all_gather | solution.py:226
  123.5 12.0 %all-gather.1 = s32[32,128]{1,0:T(8,128)S(1)} all-gather(s32[8,128]{1,0:T(8,128)S(1)} %pad_add_fusion.1), channel_id=3, replica_groups=mesh['dom_0'=8,'dom_1'=4,'dom_2'=2,'rep'=4] {'rep'}, dimensions={0}, use_global_device_ids=true | all-gather | bytes 20480 | tf_op jit(solution)/shard_map/all_gather | solution.py:226
  135.5 12.0 %all-gather.2 = f32[32,128]{1,0:T(8,128)S(1)} all-gather(f32[8,128]{1,0:T(8,128)S(1)} %pad_maximum_fusion), channel_id=4, replica_groups=mesh['dom_0'=8,'dom_1'=4,'dom_2'=2,'rep'=4] {'rep'}, dimensions={0}, use_global_device_ids=true | all-gather | bytes 20480 | tf_op jit(solution)/shard_map/all_gather | solution.py:226
  147.6 12.0 %all-gather.3 = f32[32,128]{1,0:T(8,128)S(1)} all-gather(f32[8,128]{1,0:T(8,128)S(1)} %pad_maximum_fusion.1), channel_id=5, replica_groups=mesh['dom_0'=8,'dom_1'=4,'dom_2'=2,'rep'=4] {'rep'}, dimensions={0}, use_global_device_ids=true | all-gather | bytes 20480 | tf_op jit(solution)/shard_map/all_gather | solution.py:226
  159.6 0.6 fusion
  160.2 0.6 select_select_fusion
  160.8 0.6 fusion.2
  (32 shorter events, 0.2 us)
Async XLA Ops:
  1.3 0.7 copy-start.9
  2.0 1.2 copy-start
  3.2 1.2 copy-start.1
  4.4 0.8 copy-start.2
  5.2 0.8 copy-start.3
  5.9 0.8 copy-start.4
  6.7 0.8 copy-start.5
  7.4 0.8 copy-start.6
  8.2 0.8 copy-start.7
  9.0 0.8 copy-start.8
  26.1 85.3 %collective-permute-start = (s32[2,128]{1,0:T(2,128)S(1)}, s32[2,128]{1,0:T(2,128)S(1)}, u32[]{:S(2)}, u32[]{:S(2)}) collective-permute-start(s32[2,128]{1,0:T(2,128)S(1)} %slice.103), channel_id=1, source_target_pairs={{0,4},{4,8},{8,12},{12,16},{16,20},{20,24},{24,28},{28,32},{32,36}... | collective-permute-start | bytes 3080 | tf_op jit(solution)/shard_map/ppermute | solution.py:223
  26.2 85.2 %collective-permute-start.1 = (s32[2,128]{1,0:T(2,128)S(1)}, s32[2,128]{1,0:T(2,128)S(1)}, u32[]{:S(2)}, u32[]{:S(2)}) collective-permute-start(s32[2,128]{1,0:T(2,128)S(1)} %slice.105), channel_id=1, source_target_pairs={{0,4},{4,8},{8,12},{12,16},{16,20},{20,24},{24,28},{28,32},{32,36}... | collective-permute-start | bytes 3080 | tf_op jit(solution)/shard_map/ppermute | solution.py:223
  27.9 107.6 %collective-permute-start.2 = (f32[2,128]{1,0:T(2,128)S(1)}, f32[2,128]{1,0:T(2,128)S(1)}, u32[]{:S(2)}, u32[]{:S(2)}) collective-permute-start(f32[2,128]{1,0:T(2,128)S(1)} %slice.118), channel_id=1, source_target_pairs={{0,4},{4,8},{8,12},{12,16},{16,20},{20,24},{24,28},{28,32},{32,36}... | collective-permute-start | bytes 3080 | tf_op jit(solution)/shard_map/ppermute | solution.py:223
  28.0 119.5 %collective-permute-start.3 = (f32[2,128]{1,0:T(2,128)S(1)}, f32[2,128]{1,0:T(2,128)S(1)}, u32[]{:S(2)}, u32[]{:S(2)}) collective-permute-start(f32[2,128]{1,0:T(2,128)S(1)} %slice.125), channel_id=1, source_target_pairs={{0,4},{4,8},{8,12},{12,16},{16,20},{20,24},{24,28},{28,32},{32,36}... | collective-permute-start | bytes 3080 | tf_op jit(solution)/shard_map/ppermute | solution.py:223

commit v2 on v1

v2 whole, which is shorter than its diff:
```python
import jax
import jax.numpy as jnp
from jax import lax
from jax.experimental import pallas as pl
from jax.experimental.pallas import tpu as pltpu
from jax.sharding import PartitionSpec as P

P_SIZE = 256
K = 64
LANES = 128
HIS = 10
PENALTY = 400.0
LOWEST_FILL = -1e30
FACE_LIMIT = 1073741824
KEY_LOW = -2147483648
CHUNK = 1024
F32 = jnp.float32
I32 = jnp.int32
BF16 = jnp.bfloat16
MESH = pl.DeviceIdType.MESH
DOMS = 64
REPS = 4
PLANE_DOMS = 8
PLANE = PLANE_DOMS * REPS
LAYERS = DOMS // PLANE_DOMS
GREETED = PLANE - 1 + LAYERS - 1 + REPS


def pieces(x):
    high = x.astype(BF16)
    rest = x - high.astype(F32)
    mid = rest.astype(BF16)
    low = (rest - mid.astype(F32)).astype(BF16)
    return high.astype(F32), mid.astype(F32), low.astype(F32)


def fold_rows(x, op):
    while x.shape[0] > 8:
        half = x.shape[0] // 2
        x = op(x[:half], x[half:])
    for shift in (4, 2, 1):
        x = op(x, pltpu.roll(x, shift, 0))
    return x


def combine(earlier, latter):
    prefer = (latter[1] > earlier[1]) | (latter[1] == earlier[1]) & (latter[2] < earlier[2])
    return (
        jnp.maximum(earlier[0], latter[0]),
        jnp.where(prefer, latter[1], earlier[1]),
        jnp.where(prefer, latter[2], earlier[2]),
        earlier[3] + latter[3],
    )


def kernel(
    ns_hbm, nm_hbm, sec_hbm, mst_hbm, off_hbm, qw_hbm, jac_hbm, slot_hbm, face_hbm, rank_hbm, live_ref,
    force_hbm, pen_out, face_out, gap_out, mean_out,
    ns_buf, nm_buf, sec_buf, mst_buf, off_buf, qw_buf, jac_buf, slot_buf, face_buf, rank_buf,
    force_buf, loads, table, weight, pen_by, key_by, lo_by, acc_pen, acc_key,
    plane_box, layer_box, own_f, own_i, spill_f, spill_i, got_f, got_i,
    in_sem, out_sem, plane_sem, layer_sem, own_sem, spill_sem,
):
    rows = sec_hbm.shape[1]
    chunks = rows // CHUNK
    dom, rep = lax.axis_index("dom"), lax.axis_index("rep")
    layer, spot = dom // PLANE_DOMS, (dom % PLANE_DOMS) * REPS + rep

    def plane_device(k):
        other = (spot + k) % PLANE
        return layer * PLANE_DOMS + other // REPS, other % REPS

    def layer_device(k):
        return (layer + k) % LAYERS * PLANE_DOMS + dom % PLANE_DOMS, rep

    barrier = pltpu.get_barrier_semaphore()

    def greet(device):
        pl.semaphore_signal(barrier, inc=1, device_id=device, device_id_type=MESH)

    def load(c):
        part = pl.ds(c * CHUNK, CHUNK)
        return (
            pltpu.make_async_copy(sec_hbm.at[:, part], sec_buf.at[:, part], in_sem.at[c]),
            pltpu.make_async_copy(mst_hbm.at[:, part], mst_buf.at[:, part], in_sem.at[chunks + c]),
        )

    whole = (
        (ns_hbm, ns_buf), (nm_hbm, nm_buf), (qw_hbm, qw_buf), (off_hbm, off_buf), (jac_hbm, jac_buf),
        (slot_hbm, slot_buf), (face_hbm, face_buf), (rank_hbm, rank_buf),
    )
    singles = [pltpu.make_async_copy(a, b, in_sem.at[2 * chunks + k]) for k, (a, b) in enumerate(whole)]
    for copy in singles[:3]:
        copy.start()
    for copy in load(0):
        copy.start()
    for copy in singles[3:]:
        copy.start()
    for c in range(1, chunks):
        for copy in load(c):
            copy.start()

    @pl.loop(1, PLANE)
    def _(k):
        greet(plane_device(k))

    @pl.loop(1, LAYERS)
    def _(k):
        greet(layer_device(k))

    @pl.loop(0, REPS)
    def _(k):
        greet(((dom + DOMS - 1) % DOMS, k))

    for copy in singles[:3]:
        copy.wait()
    ns = ns_buf[...]
    both = jnp.concatenate([ns.astype(F32), -nm_buf[...].astype(F32)], axis=0).T
    column = jnp.broadcast_to(qw_buf[...], (LANES, P_SIZE)).T
    weight[...] = column * (-PENALTY)
    total_weight = jnp.sum(qw_buf[...], axis=1, keepdims=True)
    coefficient = jnp.sum(both * column, axis=0, keepdims=True)
    high, mid, low = pieces(coefficient)
    eight = lax.broadcasted_iota(I32, (8, LANES), 0)
    extra = jnp.where(eight == 0, high, jnp.where(eight == 1, mid, jnp.where(eight == 2, low, 0.0)))
    lane = lax.broadcasted_iota(I32, (P_SIZE + 16, LANES), 1)
    row = lax.broadcasted_iota(I32, (P_SIZE + 16, LANES), 0)
    table[:, :LANES] = jnp.concatenate([both, extra, jnp.zeros_like(extra)], axis=0).astype(BF16)
    table[:, LANES:] = jnp.where((lane < 3) & (row < P_SIZE), 1.0, 0.0).astype(BF16)
    for copy in singles[3:]:
        copy.wait()

    live_count = live_ref[0]
    sums = jnp.zeros((48, LANES), F32)
    area = jnp.zeros((1, CHUNK), F32)
    for c in range(chunks):
        part = pl.ds(c * CHUNK, CHUNK)
        offset, jacobian = off_buf[:, part], jac_buf[:, part]
        slots = slot_buf[:, part]
        live = lax.broadcasted_iota(I32, (1, CHUNK), 1) < live_count - c * CHUNK
        for copy in load(c):
            copy.wait()
        o_high, o_mid, o_low = pieces(offset)
        sixteen = lax.broadcasted_iota(I32, (16, CHUNK), 0)
        tail = jnp.where(
            sixteen == 0, o_high, jnp.where(sixteen == 1, o_mid, jnp.where(sixteen == 2, o_low, 0.0))
        ).astype(BF16)
        data = jnp.concatenate([sec_buf[:, part], mst_buf[:, part], tail], axis=0)
        found = jnp.dot(table[:, :144], data, preferred_element_type=F32)
        gap = found[:P_SIZE]
        row_pen = -jnp.min(gap, axis=0, keepdims=True)
        row_gap = jacobian * (
            found[P_SIZE : P_SIZE + 1]
            + found[P_SIZE + 1 : P_SIZE + 2]
            + found[P_SIZE + 2 : P_SIZE + 3]
            + offset * total_weight
        )
        live_jacobian = jnp.where(live, jacobian, 0.0)
        column_weight = jnp.tile(weight[...], (1, CHUNK // LANES))
        loads[:, part] = (jnp.maximum(column_weight * gap, 0.0) * live_jacobian).astype(BF16)

        area = area + live_jacobian
        hi = jnp.where(live, lax.shift_right_logical(slots, 7), 99)
        lo = slots & (LANES - 1)
        member = sixteen == hi
        key = (rank_buf[:, part] - 2) * FACE_LIMIT + (FACE_LIMIT - 1 - face_buf[:, part])
        pens = jnp.where(member, row_pen, LOWEST_FILL)
        keys = jnp.where(member, key, KEY_LOW)
        for j in range(CHUNK // LANES):
            at = slice(j * LANES, (j + 1) * LANES)
            pen_by[c * (CHUNK // LANES) + j] = pens[:, at]
            key_by[c * (CHUNK // LANES) + j] = keys[:, at]
            lo_by[c * (CHUNK // LANES) + j] = jnp.broadcast_to(lo[:, at], (8, LANES))
        split = jnp.concatenate([jnp.where(member, piece, 0.0) for piece in pieces(row_gap)], axis=0)
        ids = lax.broadcasted_iota(I32, (LANES, CHUNK), 0)
        one_hot = jnp.where(ids == lo, 1.0, 0.0).astype(BF16)
        sums = sums + lax.dot_general(
            split.astype(BF16), one_hot, (((1,), (1,)), ((), ())), preferred_element_type=F32
        )
    seg_gap = sums[:16] + sums[16:32] + sums[32:]
    gap_total = jnp.sum(jnp.sum(seg_gap, axis=0, keepdims=True), axis=1, keepdims=True)
    area_total = jnp.sum(area, axis=1, keepdims=True) * total_weight
    first_lane = lax.broadcasted_iota(I32, (1, LANES), 1) == 0
    plane_box[spot] = jnp.where(first_lane, gap_total, area_total)

    def plane_copy(k):
        return pltpu.make_async_remote_copy(
            src_ref=plane_box.at[spot], dst_ref=plane_box.at[spot],
            send_sem=plane_sem.at[0, k], recv_sem=plane_sem.at[1, k],
            device_id=plane_device(k), device_id_type=MESH,
        )

    def layer_copy(k):
        return pltpu.make_async_remote_copy(
            src_ref=layer_box.at[layer], dst_ref=layer_box.at[layer],
            send_sem=layer_sem.at[0, k], recv_sem=layer_sem.at[1, k],
            device_id=layer_device(k), device_id_type=MESH,
        )

    pl.semaphore_wait(barrier, GREETED)

    @pl.loop(1, PLANE)
    def _(k):
        plane_copy(k).start()

    def best(first, last):
        @pl.loop(first, last)
        def _(g):
            base = pl.multiple_of(g * 8, 8)
            ids = eight + base

            def step(i, carry):
                pens, keys = carry
                mask = lo_by[i] == ids
                new_pens, new_keys = [], []
                for h in range(HIS):
                    pen = pen_by[i, pl.ds(h, 8, stride=0), :]
                    key = key_by[i, pl.ds(h, 8, stride=0), :]
                    new_pens.append(jnp.maximum(pens[h], jnp.where(mask, pen, LOWEST_FILL)))
                    new_keys.append(jnp.maximum(keys[h], jnp.where(mask, key, KEY_LOW)))
                return new_pens, new_keys

            start = (
                [jnp.full((8, LANES), LOWEST_FILL, F32)] * HIS,
                [jnp.full((8, LANES), KEY_LOW, I32)] * HIS,
            )
            pens, keys = lax.fori_loop(0, rows // LANES, step, start, unroll=2)
            for h in range(HIS):
                acc_pen[h, pl.ds(base, 8), :] = pens[h]
                acc_key[h, pl.ds(base, 8), :] = keys[h]

    best(0, 13)

    @pl.loop(1, PLANE)
    def _(k):
        plane_copy(k).wait()

    layer_box[layer] = jnp.sum(plane_box[...], axis=0)

    @pl.loop(1, LAYERS)
    def _(k):
        layer_copy(k).start()

    best(13, 16)

    for h in range(HIS):
        pen = fold_rows(acc_pen[h].T, jnp.maximum)[:1]
        key = fold_rows(acc_key[h].T, jnp.maximum)[:1]
        empty = pen <= 0.5 * LOWEST_FILL
        best_rank = jnp.where(empty, -1, lax.shift_right_arithmetic(key, 30) + 2)
        lowest_face = jnp.where(empty, FACE_LIMIT, FACE_LIMIT - 1 - (key & (FACE_LIMIT - 1)))
        if h < 8:
            own_f[rep, 0, h : h + 1, :] = pen
            own_i[rep, 0, h : h + 1, :] = best_rank
            own_i[rep, 1, h : h + 1, :] = lowest_face
        else:
            spill_f[0, h - 8 : h - 7, :] = pen
            spill_i[0, h - 8 : h - 7, :] = best_rank
            spill_i[1, h - 8 : h - 7, :] = lowest_face
    own_f[rep, 1] = seg_gap[:8]
    spill_f[1] = seg_gap[8:10]

    def own_copies(k):
        target = (dom, (rep + k) % REPS)
        return [
            pltpu.make_async_remote_copy(
                src_ref=box.at[rep], dst_ref=box.at[rep],
                send_sem=own_sem.at[0, j, k], recv_sem=own_sem.at[1, j, k],
                device_id=target, device_id_type=MESH,
            )
            for j, box in enumerate((own_f, own_i))
        ]

    def spill_copies(k):
        target = ((dom + 1) % DOMS, (rep + k) % REPS)
        return [
            pltpu.make_async_remote_copy(
                src_ref=source, dst_ref=box.at[rep],
                send_sem=spill_sem.at[0, j, k], recv_sem=spill_sem.at[1, j, k],
                device_id=target, device_id_type=MESH,
            )
            for j, (source, box) in enumerate(((spill_f, got_f), (spill_i, got_i)))
        ]

    sent = [copy for k in (2, 1, 3) for copy in own_copies(k)]
    sent += [copy for k in (2, 1, 3, 0) for copy in spill_copies(k)]
    for copy in sent:
        copy.start()

    ns = ns_buf[...]
    saved = []
    for c in range(chunks):
        part = pl.ds(c * CHUNK, CHUNK)
        force_buf[:, part] = jnp.dot(ns, loads[:, part], preferred_element_type=F32).astype(BF16)
        saved.append(pltpu.make_async_copy(force_buf.at[:, part], force_hbm.at[:, part], out_sem.at[c]))
        saved[-1].start()

    for copy in sent:
        copy.wait()

    def part_of(box_f, box_i, k):
        return box_f[k, 0], box_i[k, 0], box_i[k, 1], box_f[k, 1]

    total = part_of(own_f, own_i, 0)
    for k in range(1, REPS):
        total = combine(total, part_of(own_f, own_i, k))
    reach = part_of(got_f, got_i, 0)
    for k in range(1, REPS):
        reach = combine(reach, part_of(got_f, got_i, k))
    leading = combine([x[:2] for x in total], reach)
    for at, (pen, best_rank, face, gap_sum) in ((slice(0, 2), leading), (slice(2, 8), [x[2:] for x in total])):
        empty = best_rank < 0
        pen_out[at, :] = jnp.where(empty, 0.0, pen)
        face_out[at, :] = jnp.where(empty, -1, face)
        gap_out[at, :] = gap_sum

    @pl.loop(1, LAYERS)
    def _(k):
        layer_copy(k).wait()

    totals = jnp.sum(layer_box[...], axis=0)
    mean_out[...] = jnp.broadcast_to(totals[:, :1] / totals[:, 1:2], (1, LANES))
    for copy in saved:
        copy.wait()


def shards(ns, nm, sec, mst, off, qw, jac, slot, face, rank, live):
    rows = sec.shape[1]
    chunks = rows // CHUNK
    vmem = pl.BlockSpec(memory_space=pltpu.VMEM)
    hbm = pl.BlockSpec(memory_space=pl.ANY)
    smem = pl.BlockSpec(memory_space=pltpu.SMEM)

    def line(x):
        return x.reshape(1, -1)

    blocks = rows // LANES
    force, pen, face, gap, mean = pl.pallas_call(
        kernel,
        out_shape=(
            jax.ShapeDtypeStruct((K, rows), BF16),
            jax.ShapeDtypeStruct((8, LANES), F32),
            jax.ShapeDtypeStruct((8, LANES), I32),
            jax.ShapeDtypeStruct((8, LANES), F32),
            jax.ShapeDtypeStruct((1, LANES), F32),
        ),
        in_specs=[hbm] * 10 + [smem],
        out_specs=(hbm, vmem, vmem, vmem, vmem),
        scratch_shapes=[
            pltpu.VMEM((K, P_SIZE), BF16),
            pltpu.VMEM((K, P_SIZE), BF16),
            pltpu.VMEM((K, rows), BF16),
            pltpu.VMEM((K, rows), BF16),
            pltpu.VMEM((1, rows), F32),
            pltpu.VMEM((1, P_SIZE), F32),
            pltpu.VMEM((1, rows), F32),
            pltpu.VMEM((1, rows), I32),
            pltpu.VMEM((1, rows), I32),
            pltpu.VMEM((1, rows), I32),
            pltpu.VMEM((K, rows), BF16),
            pltpu.VMEM((P_SIZE, rows), BF16),
            pltpu.VMEM((P_SIZE + 16, 2 * LANES), BF16),
            pltpu.VMEM((P_SIZE, LANES), F32),
            pltpu.VMEM((blocks, 16, LANES), F32),
            pltpu.VMEM((blocks, 16, LANES), I32),
            pltpu.VMEM((blocks, 8, LANES), I32),
            pltpu.VMEM((HIS, LANES, LANES), F32),
            pltpu.VMEM((HIS, LANES, LANES), I32),
            pltpu.VMEM((PLANE, 1, LANES), F32),
            pltpu.VMEM((LAYERS, 1, LANES), F32),
            pltpu.VMEM((REPS, 2, 8, LANES), F32),
            pltpu.VMEM((REPS, 2, 8, LANES), I32),
            pltpu.VMEM((2, 2, LANES), F32),
            pltpu.VMEM((2, 2, LANES), I32),
            pltpu.VMEM((REPS, 2, 2, LANES), F32),
            pltpu.VMEM((REPS, 2, 2, LANES), I32),
            pltpu.SemaphoreType.DMA((2 * chunks + 8,)),
            pltpu.SemaphoreType.DMA((chunks,)),
            pltpu.SemaphoreType.DMA((2, PLANE)),
            pltpu.SemaphoreType.DMA((2, LAYERS)),
            pltpu.SemaphoreType.DMA((2, 2, REPS)),
            pltpu.SemaphoreType.DMA((2, 2, REPS)),
        ],
        compiler_params=pltpu.CompilerParams(
            vmem_limit_bytes=67_000_000, collective_id=0, has_side_effects=True
        ),
    )(ns, nm, sec, mst, line(off), line(qw), line(jac), line(slot), line(face), line(rank), live)
    return force, pen.reshape(-1), face.reshape(-1), gap.reshape(-1), mean[0, 0]


def solution(mesh):
    both = P(("dom", "rep"))
    return jax.shard_map(
        shards,
        mesh=mesh,
        in_specs=(P(), P(), P(None, ("dom", "rep")), P(None, ("dom", "rep")), both, P()) + (both,) * 5,
        out_specs=(P(None, ("dom", "rep")), P("dom"), P("dom"), P("dom"), P()),
        check_vma=False,
    )
```

time: 163 us -> 37.2 us (0.23)
  the two profiles are of different devices: /device:TPU:32 before, /device:TPU:2 now
where the time goes in v2:
time: 37.2 us; the launch traced here: 37 us
  Pallas kernels  30.3 us (81%)
  local copies, waits for them, and re-layouts  4.28 us (12%)
  between operations  2.47 us (7%)
    pallas_call x1, Pallas kernels, shards(): pl.pallas_call(kernel, out_shape=(jax.ShapeDtypeStruct((K, rows), BF16),...  30.3 us
    unnamed x12, local copies, waits for them, and re-layouts  4.28 us

profile of v2, /device:TPU:2, one launch (start us, length us, event | category | flops | bytes accessed | tf_op | source)
XLA Modules:
  0.0 37.0 jit_solution(11295195717340971036)
XLA Ops:
  1.3 30.3 %shard_map.146 = (bf16[64,8192]{1,0:T(8,128)(2,1)}, f32[8,128]{1,0:T(8,128)}, s32[8,128]{1,0:T(8,128)}, f32[8,128]{1,0:T(8,128)}, f32[1,128]{1,0:T(1,128)}) custom-call(bf16[64,256]{1,0:T(8,128)(2,1)} %ns_hbm.1, bf16[64,256]{1,0:T(8,128)(2,1)} %nm_hbm.1, bf16[64,8192]{1,0:T(8,128)(2,1)} %sec_hbm.1, bf16[64,8192]{1,0:T(8,128)(2,1)} %mst_hbm.1, ...), custom_call_target="tpu_custom_call" | custom-call | tf_op jit(solution)/shard_map/pallas_call | solution.py:338
  31.6 0.0 copy-start.2
  31.6 2.3 %copy.22 = bf16[64,8192]{1,0:T(8,128)(2,1)} copy(bf16[64,8192]{1,0:T(8,128)(2,1)} %get-tuple-element.20) | data formatting | bytes 2097152
  33.8 0.0 copy-done.2
  33.8 0.0 copy-start.1
  33.8 0.6 %copy.23 = f32[1024]{0:T(1024)} copy(f32[1024]{0:T(1024)S(1)} %bitcast.18) | data formatting | bytes 8192
  34.4 0.1 copy-done.1
  34.5 0.0 copy-start
  34.5 0.6 %copy.24 = s32[1024]{0:T(1024)} copy(s32[1024]{0:T(1024)S(1)} %bitcast.17) | data formatting | bytes 8192
  35.1 0.1 copy-done
  35.2 0.0 copy-start.3
  35.2 0.6 %copy.25 = f32[1024]{0:T(1024)} copy(f32[1024]{0:T(1024)S(1)} %bitcast.16) | data formatting | bytes 8192
  35.8 0.1 copy-done.3
Async XLA Ops:
  31.6 2.3 %copy-start.2 = (f32[8,128]{1,0:T(8,128)S(1)}, f32[8,128]{1,0:T(8,128)}, u32[]{:S(2)}) copy-start(f32[8,128]{1,0:T(8,128)} %get-tuple-element.11) | copy-start | bytes 12292
  33.8 0.7 %copy-start.1 = (s32[8,128]{1,0:T(8,128)S(1)}, s32[8,128]{1,0:T(8,128)}, u32[]{:S(2)}) copy-start(s32[8,128]{1,0:T(8,128)} %get-tuple-element.12) | copy-start | bytes 12292
  34.5 0.7 %copy-start = (f32[8,128]{1,0:T(8,128)S(1)}, f32[8,128]{1,0:T(8,128)}, u32[]{:S(2)}) copy-start(f32[8,128]{1,0:T(8,128)} %get-tuple-element.13) | copy-start | bytes 12292
  35.2 0.7 %copy-start.3 = (f32[1,128]{1,0:T(1,128)S(1)}, f32[1,128]{1,0:T(1,128)}, u32[]{:S(2)}) copy-start(f32[1,128]{1,0:T(1,128)} %get-tuple-element.14) | copy-start | bytes 1540

commit v3 on v2

v3 whole, which is shorter than its diff:
```python
import jax
import jax.numpy as jnp
from jax import lax
from jax.experimental import pallas as pl
from jax.experimental.pallas import tpu as pltpu
from jax.sharding import PartitionSpec as P

P_SIZE = 256
K = 64
LANES = 128
HIS = 10
PENALTY = 400.0
LOWEST_FILL = -1e30
FACE_LIMIT = 1073741824
FACE_FILL = 3e38
LOW_BITS = 1 << 23
CHUNK = 1024
F32 = jnp.float32
I32 = jnp.int32
BF16 = jnp.bfloat16
MESH = pl.DeviceIdType.MESH
DOMS = 64
REPS = 4
PLANE_DOMS = 8
PLANE = PLANE_DOMS * REPS
LAYERS = DOMS // PLANE_DOMS
GREETED = PLANE - 1 + LAYERS - 1 + REPS


def pieces(x):
    high = x.astype(BF16)
    rest = x - high.astype(F32)
    mid = rest.astype(BF16)
    low = (rest - mid.astype(F32)).astype(BF16)
    return high.astype(F32), mid.astype(F32), low.astype(F32)


def fold_rows(x, op):
    while x.shape[0] > 8:
        half = x.shape[0] // 2
        x = op(x[:half], x[half:])
    for shift in (4, 2, 1):
        x = op(x, pltpu.roll(x, shift, 0))
    return x


def encoded(face):
    scale = jnp.full(face.shape, 2.0**-87, F32)
    for t in range(7):
        scale = jnp.where((face & (LOW_BITS << t)) != 0, scale * 2.0 ** (1 << t), scale)
    return ((face & (LOW_BITS - 1)) + LOW_BITS).astype(F32) * scale


def decoded(value):
    top = jnp.zeros(value.shape, I32)
    for t in range(6, -1, -1):
        above = value >= 2.0 ** ((1 << t) - 64)
        value = jnp.where(above, value * 2.0 ** -(1 << t), value)
        top = jnp.where(above, top + (LOW_BITS << t), top)
    return (value * 2.0**87).astype(I32) - LOW_BITS + top


def combine(earlier, latter):
    prefer = (latter[1] > earlier[1]) | (latter[1] == earlier[1]) & (latter[2] < earlier[2])
    return (
        jnp.maximum(earlier[0], latter[0]),
        jnp.where(prefer, latter[1], earlier[1]),
        jnp.where(prefer, latter[2], earlier[2]),
        earlier[3] + latter[3],
    )


def kernel(
    ns_hbm, nm_hbm, sec_hbm, mst_hbm, off_hbm, qw_hbm, jac_hbm, slot_hbm, face_hbm, rank_hbm, live_hbm,
    force_out, pen_out, face_out, gap_out, mean_out,
    ns_buf, nm_buf, sec_buf, mst_buf, off_buf, qw_buf, jac_buf, slot_buf, face_buf, rank_buf, live_buf,
    loads, table, weight, live_jac, hi_of, lo_of, mark, rank_f, face_f, one_hot, pen_by, face_by, acc,
    plane_box, layer_box, own_f, own_i, spill_f, spill_i, got_f, got_i,
    in_sem, plane_sem, layer_sem, own_sem, spill_sem,
):
    rows = sec_hbm.shape[1]
    chunks = rows // CHUNK
    per = CHUNK // LANES
    dom, rep = lax.axis_index("dom"), lax.axis_index("rep")
    layer, spot = dom // PLANE_DOMS, (dom % PLANE_DOMS) * REPS + rep

    def plane_device(k):
        other = (spot + k) % PLANE
        return layer * PLANE_DOMS + other // REPS, other % REPS

    def layer_device(k):
        return (layer + k) % LAYERS * PLANE_DOMS + dom % PLANE_DOMS, rep

    barrier = pltpu.get_barrier_semaphore()

    def greet(device):
        pl.semaphore_signal(barrier, inc=1, device_id=device, device_id_type=MESH)

    def load(c):
        part = pl.ds(c * CHUNK, CHUNK)
        return (
            pltpu.make_async_copy(sec_hbm.at[:, part], sec_buf.at[:, part], in_sem.at[c]),
            pltpu.make_async_copy(mst_hbm.at[:, part], mst_buf.at[:, part], in_sem.at[chunks + c]),
        )

    whole = (
        (ns_hbm, ns_buf), (nm_hbm, nm_buf), (qw_hbm, qw_buf), (live_hbm, live_buf), (jac_hbm, jac_buf),
        (slot_hbm, slot_buf), (face_hbm, face_buf), (rank_hbm, rank_buf), (off_hbm, off_buf),
    )
    singles = [pltpu.make_async_copy(a, b, in_sem.at[2 * chunks + k]) for k, (a, b) in enumerate(whole)]
    for copy in singles:
        copy.start()
    for c in range(chunks):
        for copy in load(c):
            copy.start()

    @pl.loop(1, PLANE)
    def _(k):
        greet(plane_device(k))

    @pl.loop(1, LAYERS)
    def _(k):
        greet(layer_device(k))

    @pl.loop(0, REPS)
    def _(k):
        greet(((dom + DOMS - 1) % DOMS, k))

    for copy in singles[:3]:
        copy.wait()
    ns = ns_buf[...]
    both = jnp.concatenate([ns.astype(F32), -nm_buf[...].astype(F32)], axis=0).T
    column = jnp.broadcast_to(qw_buf[...], (LANES, P_SIZE)).T
    weight[...] = column * (-PENALTY)
    total_weight = jnp.sum(qw_buf[...], axis=1, keepdims=True)
    coefficient = jnp.sum(both * column, axis=0, keepdims=True)
    high, mid, low = pieces(coefficient)
    eight = lax.broadcasted_iota(I32, (8, LANES), 0)
    extra = jnp.where(eight == 0, high, jnp.where(eight == 1, mid, jnp.where(eight == 2, low, 0.0)))
    table[...] = jnp.concatenate([both, extra, jnp.zeros_like(extra)], axis=0).astype(BF16)

    for copy in singles[3:]:
        copy.wait()
    blocks = rows // LANES
    row = lax.broadcasted_iota(I32, (blocks, LANES), 0) * LANES + lax.broadcasted_iota(I32, (blocks, LANES), 1)
    live = row < live_buf[...]
    slots, ranks = slot_buf[...], rank_buf[...]
    live_jac[...] = jnp.where(live, jac_buf[...], 0.0)
    hi_of[...] = jnp.where(live, lax.shift_right_logical(slots, 7), 99)
    lo_of[...] = slots & (LANES - 1)
    mark[...] = jnp.where(ranks == 3, 2.0**28, jnp.where(ranks == 2, 2.0**14, jnp.where(ranks == 1, 1.0, 0.0)))
    rank_f[...] = ranks.astype(F32)
    face_f[...] = encoded(face_buf[...])
    area = fold_rows(live_jac[...], jnp.add)[:1]
    area_total = jnp.sum(area, axis=1, keepdims=True) * total_weight

    whole_weight = jnp.broadcast_to(total_weight, (8, LANES))
    sixteen = lax.broadcasted_iota(I32, (16, LANES), 0)
    lo_ids = lax.broadcasted_iota(I32, (LANES, LANES), 0)
    sums = jnp.zeros((64, LANES), F32)
    for c in range(chunks):
        part = pl.ds(c * CHUNK, CHUNK)
        for copy in load(c):
            copy.wait()
        data = jnp.concatenate([sec_buf[:, part], mst_buf[:, part]], axis=0)
        found = jnp.dot(table[: P_SIZE + 8], data, preferred_element_type=F32)
        splits, marks = [], []
        for j in range(per):
            i = c * per + j
            at = slice(j * LANES, (j + 1) * LANES)
            offset = off_buf[pl.ds(i, 8, stride=0), :]
            gap = found[:P_SIZE, at].reshape(P_SIZE // 8, 8, LANES) + offset[None]
            row_pen = -fold_rows(jnp.min(gap, axis=0), jnp.minimum)
            push = jnp.maximum(weight[...].reshape(P_SIZE // 8, 8, LANES) * gap, 0.0)
            push = push * live_jac[pl.ds(i, 8, stride=0), :][None]
            loads[:, pl.ds(i * LANES, LANES)] = push.reshape(P_SIZE, LANES).astype(BF16)
            linear = fold_rows(found[P_SIZE : P_SIZE + 8, at], jnp.add)
            row_gap = jac_buf[pl.ds(i, 8, stride=0), :] * (linear + offset * whole_weight)
            member = hi_of[pl.ds(i, 16, stride=0), :] == sixteen
            pen_by[i] = jnp.where(member, jnp.concatenate([row_pen, row_pen], axis=0), LOWEST_FILL)
            terms = [jnp.concatenate([p, p], axis=0) for p in pieces(row_gap)]
            terms.append(mark[pl.ds(i, 16, stride=0), :])
            splits.append(jnp.concatenate([jnp.where(member, p, 0.0) for p in terms], axis=0).astype(BF16))
            lo = lo_of[pl.ds(i, 8, stride=0), :]
            same = lo_ids.reshape(LANES // 8, 8, LANES) == lo[None]
            marks.append(jnp.where(same, 1.0, 0.0).reshape(LANES, LANES).astype(BF16))
            one_hot[:, pl.ds(i * LANES, LANES)] = marks[-1]
        sums = sums + lax.dot_general(
            jnp.concatenate(splits, axis=1), jnp.concatenate(marks, axis=1), (((1,), (1,)), ((), ())),
            preferred_element_type=F32,
        )
    seg_gap = sums[:16] + sums[16:32] + sums[32:48]
    code = sums[48:]
    best_rank = jnp.where(code >= 2.0**28, 3.0, jnp.where(code >= 2.0**14, 2.0, jnp.where(code >= 1.0, 1.0, 0.0)))
    gap_total = jnp.sum(jnp.sum(seg_gap, axis=0, keepdims=True), axis=1, keepdims=True)
    first_lane = lax.broadcasted_iota(I32, (1, LANES), 1) == 0
    plane_box[spot] = jnp.where(first_lane, gap_total, area_total)

    def plane_copy(k):
        return pltpu.make_async_remote_copy(
            src_ref=plane_box.at[spot], dst_ref=plane_box.at[spot],
            send_sem=plane_sem.at[0, k], recv_sem=plane_sem.at[1, k],
            device_id=plane_device(k), device_id_type=MESH,
        )

    def layer_copy(k):
        return pltpu.make_async_remote_copy(
            src_ref=layer_box.at[layer], dst_ref=layer_box.at[layer],
            send_sem=layer_sem.at[0, k], recv_sem=layer_sem.at[1, k],
            device_id=layer_device(k), device_id_type=MESH,
        )

    def own_copy(j, box, k):
        return pltpu.make_async_remote_copy(
            src_ref=box.at[rep], dst_ref=box.at[rep],
            send_sem=own_sem.at[0, j, k], recv_sem=own_sem.at[1, j, k],
            device_id=(dom, (rep + k) % REPS), device_id_type=MESH,
        )

    def spill_copy(j, source, box, k):
        return pltpu.make_async_remote_copy(
            src_ref=source, dst_ref=box.at[rep],
            send_sem=spill_sem.at[0, j, k], recv_sem=spill_sem.at[1, j, k],
            device_id=((dom + 1) % DOMS, (rep + k) % REPS), device_id_type=MESH,
        )

    pl.semaphore_wait(barrier, GREETED)

    @pl.loop(1, PLANE)
    def _(k):
        plane_copy(k).start()

    group = 2

    def best(source, op, fill, first, last):
        @pl.loop(first, last)
        def _(g):
            base = pl.multiple_of(g * (8 * group), 8 * group)
            ids = [eight + (base + 8 * q) for q in range(group)]

            def step(i, carry):
                lo = lo_of[pl.ds(i, 8, stride=0), :]
                masks = [lo == ids[q] for q in range(group)]
                found = []
                for h in range(HIS):
                    value = source[i, pl.ds(h, 8, stride=0), :]
                    for q in range(group):
                        found.append(op(carry[h * group + q], jnp.where(masks[q], value, fill)))
                return found

            start = [jnp.full((8, LANES), fill, F32)] * (HIS * group)
            values = lax.fori_loop(0, blocks, step, start, unroll=4)
            for h in range(HIS):
                for q in range(group):
                    acc[h, pl.ds(base + 8 * q, 8), :] = values[h * group + q]

    turns = LANES // (8 * group)
    best(pen_by, jnp.maximum, LOWEST_FILL, 0, turns)

    for c in range(chunks):
        wanted = jnp.dot(
            best_rank.astype(BF16), one_hot[:, pl.ds(c * CHUNK, CHUNK)], preferred_element_type=F32
        )
        for j in range(per):
            i = c * per + j
            member = hi_of[pl.ds(i, 16, stride=0), :] == sixteen
            member = member & (wanted[:, j * LANES : (j + 1) * LANES] == rank_f[pl.ds(i, 16, stride=0), :])
            face_by[i] = jnp.where(member, face_f[pl.ds(i, 16, stride=0), :], FACE_FILL)

    seg_pen = [fold_rows(acc[h].T, jnp.maximum)[:1] for h in range(HIS)]
    lines = [(own_f.at[rep], h) for h in range(8)] + [(spill_f, h) for h in range(2)]
    for h, (box, at) in enumerate(lines):
        box[0, at : at + 1, :] = seg_pen[h]
        box[1, at : at + 1, :] = seg_gap[h : h + 1]
        box[2, at : at + 1, :] = jnp.where(seg_pen[h] <= 0.5 * LOWEST_FILL, -1.0, best_rank[h : h + 1])

    sent = [own_copy(0, own_f, k) for k in (2, 1, 3)]
    sent += [spill_copy(0, spill_f, got_f, k) for k in (2, 1, 3, 0)]
    for copy in sent:
        copy.start()

    best(face_by, jnp.minimum, FACE_FILL, 0, turns // 2)

    @pl.loop(1, PLANE)
    def _(k):
        plane_copy(k).wait()

    layer_box[layer] = jnp.sum(plane_box[...], axis=0)

    @pl.loop(1, LAYERS)
    def _(k):
        layer_copy(k).start()

    best(face_by, jnp.minimum, FACE_FILL, turns // 2, turns)

    for h in range(HIS):
        value = fold_rows(acc[h].T, jnp.minimum)[:1]
        face = jnp.where(seg_pen[h] <= 0.5 * LOWEST_FILL, FACE_LIMIT, decoded(value))
        if h < 8:
            own_i[rep, h : h + 1, :] = face
        else:
            spill_i[h - 8 : h - 7, :] = face

    later = [own_copy(1, own_i, k) for k in (2, 1, 3)]
    later += [spill_copy(1, spill_i, got_i, k) for k in (2, 1, 3, 0)]
    for copy in later:
        copy.start()

    ns = ns_buf[...]
    for c in range(chunks):
        part = pl.ds(c * CHUNK, CHUNK)
        force_out[:, part] = jnp.dot(ns, loads[:, part], preferred_element_type=F32).astype(BF16)

    for copy in sent + later:
        copy.wait()

    def part_of(box_f, box_i, k):
        return box_f[k, 0], box_f[k, 2], box_i[k], box_f[k, 1]

    total = part_of(own_f, own_i, 0)
    for k in range(1, REPS):
        total = combine(total, part_of(own_f, own_i, k))
    reach = part_of(got_f, got_i, 0)
    for k in range(1, REPS):
        reach = combine(reach, part_of(got_f, got_i, k))
    leading = combine([x[:2] for x in total], reach)
    for at, (pen, top, face, gap_sum) in ((slice(0, 2), leading), (slice(2, 8), [x[2:] for x in total])):
        empty = top < 0.0
        pen_out[at, :] = jnp.where(empty, 0.0, pen)
        face_out[at, :] = jnp.where(empty, -1, face)
        gap_out[at, :] = gap_sum

    @pl.loop(1, LAYERS)
    def _(k):
        layer_copy(k).wait()

    totals = jnp.sum(layer_box[...], axis=0)
    mean_out[...] = jnp.broadcast_to(totals[:, :1] / totals[:, 1:2], (1, LANES))


def write_out(*refs):
    count = (len(refs) - 1) // 2
    copies = [pltpu.make_async_copy(refs[k], refs[count + k], refs[-1].at[k]) for k in range(count)]
    for copy in copies:
        copy.start()
    for copy in copies:
        copy.wait()


def shards(ns, nm, sec, mst, off, qw, jac, slot, face, rank, live):
    rows = sec.shape[1]
    chunks, blocks = rows // CHUNK, rows // LANES
    vmem = pl.BlockSpec(memory_space=pltpu.VMEM)
    hbm = pl.BlockSpec(memory_space=pl.ANY)

    def dense(x):
        return x.reshape(blocks, LANES)

    shapes = [((K, rows), BF16), ((8, LANES), F32), ((8, LANES), I32), ((8, LANES), F32), ((1, LANES), F32)]
    results = pl.pallas_call(
        kernel,
        out_shape=[pltpu.VMEM(shape, kind) for shape, kind in shapes],
        in_specs=[hbm] * 11,
        out_specs=[vmem] * 5,
        scratch_shapes=[
            pltpu.VMEM((K, P_SIZE), BF16),
            pltpu.VMEM((K, P_SIZE), BF16),
            pltpu.VMEM((K, rows), BF16),
            pltpu.VMEM((K, rows), BF16),
            pltpu.VMEM((blocks, LANES), F32),
            pltpu.VMEM((1, P_SIZE), F32),
            pltpu.VMEM((blocks, LANES), F32),
            pltpu.VMEM((blocks, LANES), I32),
            pltpu.VMEM((blocks, LANES), I32),
            pltpu.VMEM((blocks, LANES), I32),
            pltpu.VMEM((1, 1), I32),
            pltpu.VMEM((P_SIZE, rows), BF16),
            pltpu.VMEM((P_SIZE + 16, LANES), BF16),
            pltpu.VMEM((P_SIZE, LANES), F32),
            pltpu.VMEM((blocks, LANES), F32),
            pltpu.VMEM((blocks, LANES), I32),
            pltpu.VMEM((blocks, LANES), I32),
            pltpu.VMEM((blocks, LANES), F32),
            pltpu.VMEM((blocks, LANES), F32),
            pltpu.VMEM((blocks, LANES), F32),
            pltpu.VMEM((LANES, rows), BF16),
            pltpu.VMEM((blocks, 16, LANES), F32),
            pltpu.VMEM((blocks, 16, LANES), F32),
            pltpu.VMEM((HIS, LANES, LANES), F32),
            pltpu.VMEM((PLANE, 1, LANES), F32),
            pltpu.VMEM((LAYERS, 1, LANES), F32),
            pltpu.VMEM((REPS, 3, 8, LANES), F32),
            pltpu.VMEM((REPS, 8, LANES), I32),
            pltpu.VMEM((3, 2, LANES), F32),
            pltpu.VMEM((2, LANES), I32),
            pltpu.VMEM((REPS, 3, 2, LANES), F32),
            pltpu.VMEM((REPS, 2, LANES), I32),
            pltpu.SemaphoreType.DMA((2 * chunks + 9,)),
            pltpu.SemaphoreType.DMA((2, PLANE)),
            pltpu.SemaphoreType.DMA((2, LAYERS)),
            pltpu.SemaphoreType.DMA((2, 2, REPS)),
            pltpu.SemaphoreType.DMA((2, 2, REPS)),
        ],
        compiler_params=pltpu.CompilerParams(
            vmem_limit_bytes=64_000_000, collective_id=0, has_side_effects=True
        ),
    )(ns, nm, sec, mst, dense(off), qw.reshape(1, -1), dense(jac), dense(slot), dense(face), dense(rank), live.reshape(1, 1))
    force, pen, face, gap, mean = pl.pallas_call(
        write_out,
        out_shape=[jax.ShapeDtypeStruct(shape, kind) for shape, kind in shapes],
        in_specs=[vmem] * 5,
        out_specs=[hbm] * 5,
        scratch_shapes=[pltpu.SemaphoreType.DMA((5,))],
        compiler_params=pltpu.CompilerParams(vmem_limit_bytes=1 << 20),
    )(*results)
    return force, pen.reshape(-1), face.reshape(-1), gap.reshape(-1), mean[0, 0]


def solution(mesh):
    both = P(("dom", "rep"))
    return jax.shard_map(
        shards,
        mesh=mesh,
        in_specs=(P(), P(), P(None, ("dom", "rep")), P(None, ("dom", "rep")), both, P()) + (both,) * 5,
        out_specs=(P(None, ("dom", "rep")), P("dom"), P("dom"), P("dom"), P()),
        check_vma=False,
    )
```

time: 37.2 us -> 29.2 us (0.78)
  local copies, waits for them, and re-layouts: 4.28 us -> 0 us
  Pallas kernels: 30.3 us -> 27.8 us
  between operations: 2.47 us -> 1.29 us
    unnamed x12 -> x0, local copies, waits for them, and re-layouts: 4.28 us -> none
    pallas_call x1 -> x2, Pallas kernels: 30.3 us -> 27.8 us  [the longest x1 26.8 us: shards(): pl.pallas_call(kernel, out_shape=[pltpu.VMEM(shape, kind) for shape, kind...]
where the time goes in v3:
time: 29.2 us; the launch traced here: 29.1 us
  Pallas kernels  27.8 us (95%)
  between operations  1.29 us (4%)
    pallas_call x1, Pallas kernels, shards(): pl.pallas_call(kernel, out_shape=[pltpu.VMEM(shape, kind) for shape, kind...  26.8 us
    pallas_call x1, Pallas kernels, shards(): pl.pallas_call(write_out, out_shape=[jax.ShapeDtypeStruct(shape, kind) fo...  1.02 us

profile of v3, /device:TPU:2, one launch (start us, length us, event | category | flops | bytes accessed | tf_op | source)
XLA Modules:
  0.0 29.1 jit_solution(3408724885986000288)
XLA Ops:
  1.3 26.8 %shard_map.146 = (bf16[64,8192]{1,0:T(8,128)(2,1)S(1)}, f32[8,128]{1,0:T(8,128)S(1)}, s32[8,128]{1,0:T(8,128)S(1)}, f32[8,128]{1,0:T(8,128)S(1)}, f32[1,128]{1,0:T(1,128)S(1)}) custom-call(bf16[64,256]{1,0:T(8,128)(2,1)} %ns_hbm.1, bf16[64,256]{1,0:T(8,128)(2,1)} %nm_hbm.1, bf16[64,8192]{1,0:T(8,128)(2,1)} %sec_hbm.1, bf16[64,8192]{1,0:T(8,128)(2,1)} %mst_hbm.1, ...), custom_call_target="tpu_custom_call" | custom-call | tf_op jit(solution)/shard_map/pallas_call | solution.py:360
  28.1 1.0 %shard_map.147 = (bf16[64,8192]{1,0:T(8,128)(2,1)}, f32[8,128]{1,0:T(8,128)}, s32[8,128]{1,0:T(8,128)}, f32[8,128]{1,0:T(8,128)}, f32[1,128]{1,0:T(1,128)}) custom-call(bf16[64,8192]{1,0:T(8,128)(2,1)S(1)} %get-tuple-element.15.refs_0_, f32[8,128]{1,0:T(8,128)S(1)} %get-tuple-element.16.refs_1_, s32[8,128]{1,0:T(8,128)S(1)} %get-tuple-element.17.refs_2_, ...), custom_call_target="tpu_custom_call" | custom-call | tf_op jit(solution)/shard_map/pallas_call | solution.py:408

commit v4 on v3

--- a/solution.py
+++ b/solution.py
@@ -74,7 +74,7 @@
     ns_hbm, nm_hbm, sec_hbm, mst_hbm, off_hbm, qw_hbm, jac_hbm, slot_hbm, face_hbm, rank_hbm, live_hbm,
     force_out, pen_out, face_out, gap_out, mean_out,
     ns_buf, nm_buf, sec_buf, mst_buf, off_buf, qw_buf, jac_buf, slot_buf, face_buf, rank_buf, live_buf,
-    loads, table, weight, live_jac, hi_of, lo_of, mark, rank_f, face_f, one_hot, pen_by, face_by, acc,
+    table, weight, live_jac, hi_of, lo_of, lo_f, mark, rank_f, face_f, one_hot, pen_by, face_by, acc,
     plane_box, layer_box, own_f, own_i, spill_f, spill_i, got_f, got_i,
     in_sem, plane_sem, layer_sem, own_sem, spill_sem,
 ):
@@ -82,14 +82,14 @@
     chunks = rows // CHUNK
     per = CHUNK // LANES
     dom, rep = lax.axis_index("dom"), lax.axis_index("rep")
-    layer, spot = dom // PLANE_DOMS, (dom % PLANE_DOMS) * REPS + rep
+    layer, spot = dom >> 3, (dom & 7) * REPS + rep
 
     def plane_device(k):
-        other = (spot + k) % PLANE
-        return layer * PLANE_DOMS + other // REPS, other % REPS
+        other = (spot + k) & (PLANE - 1)
+        return layer * PLANE_DOMS + (other >> 2), other & 3
 
     def layer_device(k):
-        return (layer + k) % LAYERS * PLANE_DOMS + dom % PLANE_DOMS, rep
+        return ((layer + k) & (LAYERS - 1)) * PLANE_DOMS + (dom & 7), rep
 
     barrier = pltpu.get_barrier_semaphore()
 
@@ -124,7 +124,7 @@
 
     @pl.loop(0, REPS)
     def _(k):
-        greet(((dom + DOMS - 1) % DOMS, k))
+        greet(((dom + DOMS - 1) & (DOMS - 1), k))
 
     for copy in singles[:3]:
         copy.wait()
@@ -148,6 +148,7 @@
     live_jac[...] = jnp.where(live, jac_buf[...], 0.0)
     hi_of[...] = jnp.where(live, lax.shift_right_logical(slots, 7), 99)
     lo_of[...] = slots & (LANES - 1)
+    lo_f[...] = (slots & (LANES - 1)).astype(F32)
     mark[...] = jnp.where(ranks == 3, 2.0**28, jnp.where(ranks == 2, 2.0**14, jnp.where(ranks == 1, 1.0, 0.0)))
     rank_f[...] = ranks.astype(F32)
     face_f[...] = encoded(face_buf[...])
@@ -156,24 +157,28 @@
 
     whole_weight = jnp.broadcast_to(total_weight, (8, LANES))
     sixteen = lax.broadcasted_iota(I32, (16, LANES), 0)
-    lo_ids = lax.broadcasted_iota(I32, (LANES, LANES), 0)
+    lo_ids = lax.broadcasted_iota(I32, (LANES, LANES), 0).astype(F32).astype(BF16)
     sums = jnp.zeros((64, LANES), F32)
     for c in range(chunks):
-        part = pl.ds(c * CHUNK, CHUNK)
         for copy in load(c):
             copy.wait()
+
+    def project(c, width, count):
+        part = pl.ds(c * width, width)
         data = jnp.concatenate([sec_buf[:, part], mst_buf[:, part]], axis=0)
-        found = jnp.dot(table[: P_SIZE + 8], data, preferred_element_type=F32)
+        return jnp.dot(table[:count], data, preferred_element_type=F32)
+
+    ahead = project(0, CHUNK, P_SIZE + 8)
+    for c in range(chunks):
+        found = ahead
+        if c + 1 < chunks:
+            ahead = project(c + 1, CHUNK, P_SIZE + 8)
         splits, marks = [], []
         for j in range(per):
             i = c * per + j
             at = slice(j * LANES, (j + 1) * LANES)
             offset = off_buf[pl.ds(i, 8, stride=0), :]
-            gap = found[:P_SIZE, at].reshape(P_SIZE // 8, 8, LANES) + offset[None]
-            row_pen = -fold_rows(jnp.min(gap, axis=0), jnp.minimum)
-            push = jnp.maximum(weight[...].reshape(P_SIZE // 8, 8, LANES) * gap, 0.0)
-            push = push * live_jac[pl.ds(i, 8, stride=0), :][None]
-            loads[:, pl.ds(i * LANES, LANES)] = push.reshape(P_SIZE, LANES).astype(BF16)
+            row_pen = -(fold_rows(found[:P_SIZE, at], jnp.minimum) + offset)
             linear = fold_rows(found[P_SIZE : P_SIZE + 8, at], jnp.add)
             row_gap = jac_buf[pl.ds(i, 8, stride=0), :] * (linear + offset * whole_weight)
             member = hi_of[pl.ds(i, 16, stride=0), :] == sixteen
@@ -181,9 +186,9 @@
             terms = [jnp.concatenate([p, p], axis=0) for p in pieces(row_gap)]
             terms.append(mark[pl.ds(i, 16, stride=0), :])
             splits.append(jnp.concatenate([jnp.where(member, p, 0.0) for p in terms], axis=0).astype(BF16))
-            lo = lo_of[pl.ds(i, 8, stride=0), :]
-            same = lo_ids.reshape(LANES // 8, 8, LANES) == lo[None]
-            marks.append(jnp.where(same, 1.0, 0.0).reshape(LANES, LANES).astype(BF16))
+            lo = lo_f[pl.ds(i, 16, stride=0), :].astype(BF16)
+            same = lo_ids.reshape(LANES // 16, 16, LANES) == lo[None]
+            marks.append(jnp.where(same, jnp.bfloat16(1), jnp.bfloat16(0)).reshape(LANES, LANES))
             one_hot[:, pl.ds(i * LANES, LANES)] = marks[-1]
         sums = sums + lax.dot_general(
             jnp.concatenate(splits, axis=1), jnp.concatenate(marks, axis=1), (((1,), (1,)), ((), ())),
@@ -214,14 +219,14 @@
         return pltpu.make_async_remote_copy(
             src_ref=box.at[rep], dst_ref=box.at[rep],
             send_sem=own_sem.at[0, j, k], recv_sem=own_sem.at[1, j, k],
-            device_id=(dom, (rep + k) % REPS), device_id_type=MESH,
+            device_id=(dom, (rep + k) & (REPS - 1)), device_id_type=MESH,
         )
 
     def spill_copy(j, source, box, k):
         return pltpu.make_async_remote_copy(
             src_ref=source, dst_ref=box.at[rep],
             send_sem=spill_sem.at[0, j, k], recv_sem=spill_sem.at[1, j, k],
-            device_id=((dom + 1) % DOMS, (rep + k) % REPS), device_id_type=MESH,
+            device_id=((dom + 1) & (DOMS - 1), (rep + k) & (REPS - 1)), device_id_type=MESH,
         )
 
     pl.semaphore_wait(barrier, GREETED)
@@ -249,7 +254,7 @@
                 return found
 
             start = [jnp.full((8, LANES), fill, F32)] * (HIS * group)
-            values = lax.fori_loop(0, blocks, step, start, unroll=4)
+            values = lax.fori_loop(0, blocks, step, start, unroll=8)
             for h in range(HIS):
                 for q in range(group):
                     acc[h, pl.ds(base + 8 * q, 8), :] = values[h * group + q]
@@ -307,9 +312,30 @@
         copy.start()
 
     ns = ns_buf[...]
-    for c in range(chunks):
-        part = pl.ds(c * CHUNK, CHUNK)
-        force_out[:, part] = jnp.dot(ns, loads[:, part], preferred_element_type=F32).astype(BF16)
+    half = 256
+    ns = ns_buf[...]
+    turns_of = rows // half
+
+    def push_of(c, found):
+        pushes = []
+        for j in range(half // LANES):
+            i = c * (half // LANES) + j
+            gap = found[:, j * LANES : (j + 1) * LANES].reshape(P_SIZE // 8, 8, LANES)
+            gap = gap + off_buf[pl.ds(i, 8, stride=0), :][None]
+            push = jnp.maximum(weight[...].reshape(P_SIZE // 8, 8, LANES) * gap, 0.0)
+            push = push * live_jac[pl.ds(i, 8, stride=0), :][None]
+            pushes.append(push.reshape(P_SIZE, LANES).astype(BF16))
+        return jnp.concatenate(pushes, axis=1)
+
+    ahead, ready = project(0, half, P_SIZE), None
+    for c in range(turns_of + 1):
+        now = ahead
+        if c + 1 < turns_of:
+            ahead = project(c + 1, half, P_SIZE)
+        if ready is not None:
+            force_out[:, pl.ds((c - 1) * half, half)] = jnp.dot(ns, ready, preferred_element_type=F32).astype(BF16)
+        if c < turns_of:
+            ready = push_of(c, now)
 
     for copy in sent + later:
         copy.wait()
@@ -374,12 +400,12 @@
             pltpu.VMEM((blocks, LANES), I32),
             pltpu.VMEM((blocks, LANES), I32),
             pltpu.VMEM((1, 1), I32),
-            pltpu.VMEM((P_SIZE, rows), BF16),
             pltpu.VMEM((P_SIZE + 16, LANES), BF16),
             pltpu.VMEM((P_SIZE, LANES), F32),
             pltpu.VMEM((blocks, LANES), F32),
             pltpu.VMEM((blocks, LANES), I32),
             pltpu.VMEM((blocks, LANES), I32),
+            pltpu.VMEM((blocks, LANES), F32),
             pltpu.VMEM((blocks, LANES), F32),
             pltpu.VMEM((blocks, LANES), F32),
             pltpu.VMEM((blocks, LANES), F32),

time: 29.2 us -> 26.2 us (0.90)
  Pallas kernels: 27.8 us -> 24.8 us
    pallas_call x1, Pallas kernels: 26.8 us -> 23.8 us  [shards(): pl.pallas_call(kernel, out_shape=[pltpu.VMEM(shape, kind) for shape, kind...]
where the time goes in v4:
time: 26.2 us; the launch traced here: 26.1 us
  Pallas kernels  24.8 us (95%)
  between operations  1.29 us (5%)
    pallas_call x1, Pallas kernels, shards(): pl.pallas_call(kernel, out_shape=[pltpu.VMEM(shape, kind) for shape, kind...  23.8 us
    pallas_call x1, Pallas kernels, shards(): pl.pallas_call(write_out, out_shape=[jax.ShapeDtypeStruct(shape, kind) fo...  1.02 us

profile of v4, /device:TPU:2, one launch (start us, length us, event | category | flops | bytes accessed | tf_op | source)
XLA Modules:
  0.0 26.1 jit_solution(363704369696287344)
XLA Ops:
  1.3 23.8 %shard_map.146 = (bf16[64,8192]{1,0:T(8,128)(2,1)S(1)}, f32[8,128]{1,0:T(8,128)S(1)}, s32[8,128]{1,0:T(8,128)S(1)}, f32[8,128]{1,0:T(8,128)S(1)}, f32[1,128]{1,0:T(1,128)S(1)}) custom-call(bf16[64,256]{1,0:T(8,128)(2,1)} %ns_hbm.1, bf16[64,256]{1,0:T(8,128)(2,1)} %nm_hbm.1, bf16[64,8192]{1,0:T(8,128)(2,1)} %sec_hbm.1, bf16[64,8192]{1,0:T(8,128)(2,1)} %mst_hbm.1, ...), custom_call_target="tpu_custom_call" | custom-call | tf_op jit(solution)/shard_map/pallas_call | solution.py:386
  25.1 1.0 %shard_map.147 = (bf16[64,8192]{1,0:T(8,128)(2,1)}, f32[8,128]{1,0:T(8,128)}, s32[8,128]{1,0:T(8,128)}, f32[8,128]{1,0:T(8,128)}, f32[1,128]{1,0:T(1,128)}) custom-call(bf16[64,8192]{1,0:T(8,128)(2,1)S(1)} %get-tuple-element.15.refs_0_, f32[8,128]{1,0:T(8,128)S(1)} %get-tuple-element.16.refs_1_, s32[8,128]{1,0:T(8,128)S(1)} %get-tuple-element.17.refs_2_, ...), custom_call_target="tpu_custom_call" | custom-call | tf_op jit(solution)/shard_map/pallas_call | solution.py:434

commit v5 on v4

--- a/solution.py
+++ b/solution.py
@@ -15,6 +15,7 @@
 FACE_FILL = 3e38
 LOW_BITS = 1 << 23
 CHUNK = 1024
+PARTS = 2
 F32 = jnp.float32
 I32 = jnp.int32
 BF16 = jnp.bfloat16
@@ -74,7 +75,7 @@
     ns_hbm, nm_hbm, sec_hbm, mst_hbm, off_hbm, qw_hbm, jac_hbm, slot_hbm, face_hbm, rank_hbm, live_hbm,
     force_out, pen_out, face_out, gap_out, mean_out,
     ns_buf, nm_buf, sec_buf, mst_buf, off_buf, qw_buf, jac_buf, slot_buf, face_buf, rank_buf, live_buf,
-    table, weight, live_jac, hi_of, lo_of, lo_f, mark, rank_f, face_f, one_hot, pen_by, face_by, acc,
+    table, weight, live_jac, hi_of, lo_of, lo_f, mark, rank_f, face_f, one_hot, pen_by, face_by, acc_pen, acc_face,
     plane_box, layer_box, own_f, own_i, spill_f, spill_i, got_f, got_i,
     in_sem, plane_sem, layer_sem, own_sem, spill_sem,
 ):
@@ -97,30 +98,30 @@
         pl.semaphore_signal(barrier, inc=1, device_id=device, device_id_type=MESH)
 
     def load(c):
-        part = pl.ds(c * CHUNK, CHUNK)
+        part = pl.ds(c * (rows // PARTS), rows // PARTS)
         return (
             pltpu.make_async_copy(sec_hbm.at[:, part], sec_buf.at[:, part], in_sem.at[c]),
-            pltpu.make_async_copy(mst_hbm.at[:, part], mst_buf.at[:, part], in_sem.at[chunks + c]),
+            pltpu.make_async_copy(mst_hbm.at[:, part], mst_buf.at[:, part], in_sem.at[PARTS + c]),
         )
 
     whole = (
         (ns_hbm, ns_buf), (nm_hbm, nm_buf), (qw_hbm, qw_buf), (live_hbm, live_buf), (jac_hbm, jac_buf),
         (slot_hbm, slot_buf), (face_hbm, face_buf), (rank_hbm, rank_buf), (off_hbm, off_buf),
     )
-    singles = [pltpu.make_async_copy(a, b, in_sem.at[2 * chunks + k]) for k, (a, b) in enumerate(whole)]
+    singles = [pltpu.make_async_copy(a, b, in_sem.at[2 * PARTS + k]) for k, (a, b) in enumerate(whole)]
+    @pl.loop(1, LAYERS)
+    def _(k):
+        greet(layer_device(k))
+
     for copy in singles:
         copy.start()
-    for c in range(chunks):
+    for c in range(PARTS):
         for copy in load(c):
             copy.start()
 
     @pl.loop(1, PLANE)
     def _(k):
         greet(plane_device(k))
-
-    @pl.loop(1, LAYERS)
-    def _(k):
-        greet(layer_device(k))
 
     @pl.loop(0, REPS)
     def _(k):
@@ -159,7 +160,7 @@
     sixteen = lax.broadcasted_iota(I32, (16, LANES), 0)
     lo_ids = lax.broadcasted_iota(I32, (LANES, LANES), 0).astype(F32).astype(BF16)
     sums = jnp.zeros((64, LANES), F32)
-    for c in range(chunks):
+    for c in range(PARTS):
         for copy in load(c):
             copy.wait()
 
@@ -235,10 +236,8 @@
     def _(k):
         plane_copy(k).start()
 
-    group = 2
-
-    def best(source, op, fill, first, last):
-        @pl.loop(first, last)
+    def search(jobs, his, group):
+        @pl.loop(0, LANES // (8 * group))
         def _(g):
             base = pl.multiple_of(g * (8 * group), 8 * group)
             ids = [eight + (base + 8 * q) for q in range(group)]
@@ -247,20 +246,23 @@
                 lo = lo_of[pl.ds(i, 8, stride=0), :]
                 masks = [lo == ids[q] for q in range(group)]
                 found = []
-                for h in range(HIS):
-                    value = source[i, pl.ds(h, 8, stride=0), :]
+                for source, op, fill, _ in jobs:
+                    for h in his:
+                        value = source[i, pl.ds(h, 8, stride=0), :]
+                        for mask in masks:
+                            found.append(op(carry[len(found)], jnp.where(mask, value, fill)))
+                return found
+
+            start = [jnp.full((8, LANES), fill, F32) for _, _, fill, _ in jobs for _ in range(len(his) * group)]
+            values = iter(lax.fori_loop(0, blocks, step, start, unroll=16))
+            for _, _, _, acc in jobs:
+                for h in his:
                     for q in range(group):
-                        found.append(op(carry[h * group + q], jnp.where(masks[q], value, fill)))
-                return found
-
-            start = [jnp.full((8, LANES), fill, F32)] * (HIS * group)
-            values = lax.fori_loop(0, blocks, step, start, unroll=8)
-            for h in range(HIS):
-                for q in range(group):
-                    acc[h, pl.ds(base + 8 * q, 8), :] = values[h * group + q]
-
-    turns = LANES // (8 * group)
-    best(pen_by, jnp.maximum, LOWEST_FILL, 0, turns)
+                        acc[h, pl.ds(base + 8 * q, 8), :] = next(values)
+
+    pen_job = (pen_by, jnp.maximum, LOWEST_FILL, acc_pen)
+    face_job = (face_by, jnp.minimum, FACE_FILL, acc_face)
+    own_his, spill_his = tuple(range(8)), (8, 9)
 
     for c in range(chunks):
         wanted = jnp.dot(
@@ -272,19 +274,33 @@
             member = member & (wanted[:, j * LANES : (j + 1) * LANES] == rank_f[pl.ds(i, 16, stride=0), :])
             face_by[i] = jnp.where(member, face_f[pl.ds(i, 16, stride=0), :], FACE_FILL)
 
-    seg_pen = [fold_rows(acc[h].T, jnp.maximum)[:1] for h in range(HIS)]
-    lines = [(own_f.at[rep], h) for h in range(8)] + [(spill_f, h) for h in range(2)]
-    for h, (box, at) in enumerate(lines):
-        box[0, at : at + 1, :] = seg_pen[h]
-        box[1, at : at + 1, :] = seg_gap[h : h + 1]
-        box[2, at : at + 1, :] = jnp.where(seg_pen[h] <= 0.5 * LOWEST_FILL, -1.0, best_rank[h : h + 1])
-
-    sent = [own_copy(0, own_f, k) for k in (2, 1, 3)]
-    sent += [spill_copy(0, spill_f, got_f, k) for k in (2, 1, 3, 0)]
+    seg_pen = {}
+
+    def settle_pens(his, box):
+        for at, h in enumerate(his):
+            seg_pen[h] = fold_rows(acc_pen[h].T, jnp.maximum)[:1]
+            box[0, at : at + 1, :] = seg_pen[h]
+            box[1, at : at + 1, :] = seg_gap[h : h + 1]
+            box[2, at : at + 1, :] = jnp.where(seg_pen[h] <= 0.5 * LOWEST_FILL, -1.0, best_rank[h : h + 1])
+
+    def settle_faces(his, box):
+        for at, h in enumerate(his):
+            value = fold_rows(acc_face[h].T, jnp.minimum)[:1]
+            box[at : at + 1, :] = jnp.where(seg_pen[h] <= 0.5 * LOWEST_FILL, FACE_LIMIT, decoded(value))
+
+    search([pen_job, face_job], spill_his, 4)
+    settle_pens(spill_his, spill_f)
+    settle_faces(spill_his, spill_i)
+    sent = [spill_copy(0, spill_f, got_f, k) for k in (2, 1, 3, 0)]
+    sent += [spill_copy(1, spill_i, got_i, k) for k in (2, 1, 3, 0)]
     for copy in sent:
         copy.start()
 
-    best(face_by, jnp.minimum, FACE_FILL, 0, turns // 2)
+    search([pen_job], own_his, 2)
+    settle_pens(own_his, own_f.at[rep])
+    middle = [own_copy(0, own_f, k) for k in (2, 1, 3)]
+    for copy in middle:
+        copy.start()
 
     @pl.loop(1, PLANE)
     def _(k):
@@ -296,22 +312,13 @@
     def _(k):
         layer_copy(k).start()
 
-    best(face_by, jnp.minimum, FACE_FILL, turns // 2, turns)
-
-    for h in range(HIS):
-        value = fold_rows(acc[h].T, jnp.minimum)[:1]
-        face = jnp.where(seg_pen[h] <= 0.5 * LOWEST_FILL, FACE_LIMIT, decoded(value))
-        if h < 8:
-            own_i[rep, h : h + 1, :] = face
-        else:
-            spill_i[h - 8 : h - 7, :] = face
-
+    search([face_job], own_his, 2)
+    settle_faces(own_his, own_i.at[rep])
     later = [own_copy(1, own_i, k) for k in (2, 1, 3)]
-    later += [spill_copy(1, spill_i, got_i, k) for k in (2, 1, 3, 0)]
     for copy in later:
         copy.start()
-
-    ns = ns_buf[...]
+    sent += middle
+
     half = 256
     ns = ns_buf[...]
     turns_of = rows // half
@@ -413,6 +420,7 @@
             pltpu.VMEM((blocks, 16, LANES), F32),
             pltpu.VMEM((blocks, 16, LANES), F32),
             pltpu.VMEM((HIS, LANES, LANES), F32),
+            pltpu.VMEM((HIS, LANES, LANES), F32),
             pltpu.VMEM((PLANE, 1, LANES), F32),
             pltpu.VMEM((LAYERS, 1, LANES), F32),
             pltpu.VMEM((REPS, 3, 8, LANES), F32),
@@ -421,7 +429,7 @@
             pltpu.VMEM((2, LANES), I32),
             pltpu.VMEM((REPS, 3, 2, LANES), F32),
             pltpu.VMEM((REPS, 2, LANES), I32),
-            pltpu.SemaphoreType.DMA((2 * chunks + 9,)),
+            pltpu.SemaphoreType.DMA((2 * PARTS + 9,)),
             pltpu.SemaphoreType.DMA((2, PLANE)),
             pltpu.SemaphoreType.DMA((2, LAYERS)),
             pltpu.SemaphoreType.DMA((2, 2, REPS)),

time: 26.2 us -> 24.9 us (0.950)
  the two profiles are of different devices: /device:TPU:2 before, /device:TPU:1 now
where the time goes in v5:
time: 24.9 us; the launch traced here: 24.8 us
  Pallas kernels  23.5 us (94%)
  between operations  1.29 us (5%)
    pallas_call x1, Pallas kernels, shards(): pl.pallas_call(kernel, out_shape=[pltpu.VMEM(shape, kind) for shape, kind...  22.5 us
    pallas_call x1, Pallas kernels, shards(): pl.pallas_call(write_out, out_shape=[jax.ShapeDtypeStruct(shape, kind) fo...  1.02 us

profile of v5, /device:TPU:1, one launch (start us, length us, event | category | flops | bytes accessed | tf_op | source)
XLA Modules:
  0.0 24.8 jit_solution(2966756242813472074)
XLA Ops:
  1.3 22.5 %shard_map.146 = (bf16[64,8192]{1,0:T(8,128)(2,1)S(1)}, f32[8,128]{1,0:T(8,128)S(1)}, s32[8,128]{1,0:T(8,128)S(1)}, f32[8,128]{1,0:T(8,128)S(1)}, f32[1,128]{1,0:T(1,128)S(1)}) custom-call(bf16[64,256]{1,0:T(8,128)(2,1)} %ns_hbm.1, bf16[64,256]{1,0:T(8,128)(2,1)} %nm_hbm.1, bf16[64,8192]{1,0:T(8,128)(2,1)} %sec_hbm.1, bf16[64,8192]{1,0:T(8,128)(2,1)} %mst_hbm.1, ...), custom_call_target="tpu_custom_call" | custom-call | tf_op jit(solution)/shard_map/pallas_call | solution.py:393
  23.8 1.0 %shard_map.147 = (bf16[64,8192]{1,0:T(8,128)(2,1)}, f32[8,128]{1,0:T(8,128)}, s32[8,128]{1,0:T(8,128)}, f32[8,128]{1,0:T(8,128)}, f32[1,128]{1,0:T(1,128)}) custom-call(bf16[64,8192]{1,0:T(8,128)(2,1)S(1)} %get-tuple-element.15.refs_0_, f32[8,128]{1,0:T(8,128)S(1)} %get-tuple-element.16.refs_1_, s32[8,128]{1,0:T(8,128)S(1)} %get-tuple-element.17.refs_2_, ...), custom_call_target="tpu_custom_call" | custom-call | tf_op jit(solution)/shard_map/pallas_call | solution.py:442

commit v6 on v5

--- a/solution.py
+++ b/solution.py
@@ -160,6 +160,7 @@
     sixteen = lax.broadcasted_iota(I32, (16, LANES), 0)
     lo_ids = lax.broadcasted_iota(I32, (LANES, LANES), 0).astype(F32).astype(BF16)
     sums = jnp.zeros((64, LANES), F32)
+    live_gap = jnp.zeros((8, LANES), F32)
     for c in range(PARTS):
         for copy in load(c):
             copy.wait()
@@ -181,7 +182,9 @@
             offset = off_buf[pl.ds(i, 8, stride=0), :]
             row_pen = -(fold_rows(found[:P_SIZE, at], jnp.minimum) + offset)
             linear = fold_rows(found[P_SIZE : P_SIZE + 8, at], jnp.add)
-            row_gap = jac_buf[pl.ds(i, 8, stride=0), :] * (linear + offset * whole_weight)
+            linear = linear + offset * whole_weight
+            row_gap = jac_buf[pl.ds(i, 8, stride=0), :] * linear
+            live_gap = live_gap + live_jac[pl.ds(i, 8, stride=0), :] * linear
             member = hi_of[pl.ds(i, 16, stride=0), :] == sixteen
             pen_by[i] = jnp.where(member, jnp.concatenate([row_pen, row_pen], axis=0), LOWEST_FILL)
             terms = [jnp.concatenate([p, p], axis=0) for p in pieces(row_gap)]
@@ -198,7 +201,7 @@
     seg_gap = sums[:16] + sums[16:32] + sums[32:48]
     code = sums[48:]
     best_rank = jnp.where(code >= 2.0**28, 3.0, jnp.where(code >= 2.0**14, 2.0, jnp.where(code >= 1.0, 1.0, 0.0)))
-    gap_total = jnp.sum(jnp.sum(seg_gap, axis=0, keepdims=True), axis=1, keepdims=True)
+    gap_total = jnp.sum(live_gap[:1], axis=1, keepdims=True)
     first_lane = lax.broadcasted_iota(I32, (1, LANES), 1) == 0
     plane_box[spot] = jnp.where(first_lane, gap_total, area_total)
 
@@ -236,8 +239,8 @@
     def _(k):
         plane_copy(k).start()
 
-    def search(jobs, his, group):
-        @pl.loop(0, LANES // (8 * group))
+    def search(jobs, his, group, first=0, last=None):
+        @pl.loop(first, LANES // (8 * group) if last is None else last)
         def _(g):
             base = pl.multiple_of(g * (8 * group), 8 * group)
             ids = [eight + (base + 8 * q) for q in range(group)]
@@ -302,6 +305,8 @@
     for copy in middle:
         copy.start()
 
+    search([face_job], own_his, 2, 0, 1)
+
     @pl.loop(1, PLANE)
     def _(k):
         plane_copy(k).wait()
@@ -312,7 +317,7 @@
     def _(k):
         layer_copy(k).start()
 
-    search([face_job], own_his, 2)
+    search([face_job], own_his, 2, 1)
     settle_faces(own_his, own_i.at[rep])
     later = [own_copy(1, own_i, k) for k in (2, 1, 3)]
     for copy in later:

time: 24.9 us -> 24.6 us (0.988)
  Pallas kernels: 23.5 us -> 23.2 us
    pallas_call x1, Pallas kernels: 22.5 us -> 22.2 us  [shards(): pl.pallas_call(kernel, out_shape=[pltpu.VMEM(shape, kind) for shape, kind...]
where the time goes in v6:
time: 24.6 us; the launch traced here: 24.5 us
  Pallas kernels  23.2 us (94%)
  between operations  1.29 us (5%)
    pallas_call x1, Pallas kernels, shards(): pl.pallas_call(kernel, out_shape=[pltpu.VMEM(shape, kind) for shape, kind...  22.2 us
    pallas_call x1, Pallas kernels, shards(): pl.pallas_call(write_out, out_shape=[jax.ShapeDtypeStruct(shape, kind) fo...  1.02 us

profile of v6, /device:TPU:1, one launch (start us, length us, event | category | flops | bytes accessed | tf_op | source)
XLA Modules:
  0.0 24.5 jit_solution(2115369883697243828)
XLA Ops:
  1.3 22.2 %shard_map.146 = (bf16[64,8192]{1,0:T(8,128)(2,1)S(1)}, f32[8,128]{1,0:T(8,128)S(1)}, s32[8,128]{1,0:T(8,128)S(1)}, f32[8,128]{1,0:T(8,128)S(1)}, f32[1,128]{1,0:T(1,128)S(1)}) custom-call(bf16[64,256]{1,0:T(8,128)(2,1)} %ns_hbm.1, bf16[64,256]{1,0:T(8,128)(2,1)} %nm_hbm.1, bf16[64,8192]{1,0:T(8,128)(2,1)} %sec_hbm.1, bf16[64,8192]{1,0:T(8,128)(2,1)} %mst_hbm.1, ...), custom_call_target="tpu_custom_call" | custom-call | tf_op jit(solution)/shard_map/pallas_call | solution.py:398
  23.4 1.0 %shard_map.147 = (bf16[64,8192]{1,0:T(8,128)(2,1)}, f32[8,128]{1,0:T(8,128)}, s32[8,128]{1,0:T(8,128)}, f32[8,128]{1,0:T(8,128)}, f32[1,128]{1,0:T(1,128)}) custom-call(bf16[64,8192]{1,0:T(8,128)(2,1)S(1)} %get-tuple-element.15.refs_0_, f32[8,128]{1,0:T(8,128)S(1)} %get-tuple-element.16.refs_1_, s32[8,128]{1,0:T(8,128)S(1)} %get-tuple-element.17.refs_2_, ...), custom_call_target="tpu_custom_call" | custom-call | tf_op jit(solution)/shard_map/pallas_call | solution.py:447

commit v7 on v6

--- a/solution.py
+++ b/solution.py
@@ -257,7 +257,7 @@
                 return found
 
             start = [jnp.full((8, LANES), fill, F32) for _, _, fill, _ in jobs for _ in range(len(his) * group)]
-            values = iter(lax.fori_loop(0, blocks, step, start, unroll=16))
+            values = iter(lax.fori_loop(0, blocks, step, start, unroll=32))
             for _, _, _, acc in jobs:
                 for h in his:
                     for q in range(group):

time: 24.6 us -> 24.5 us (level)
  no operation moved by 1% of the time
where the time goes in v7:
time: 24.5 us; the launch traced here: 24.4 us
  Pallas kernels  23.1 us (94%)
  between operations  1.29 us (5%)
    pallas_call x1, Pallas kernels, shards(): pl.pallas_call(kernel, out_shape=[pltpu.VMEM(shape, kind) for shape, kind...  22.1 us
    pallas_call x1, Pallas kernels, shards(): pl.pallas_call(write_out, out_shape=[jax.ShapeDtypeStruct(shape, kind) fo...  1.02 us

profile of v7, /device:TPU:1, one launch (start us, length us, event | category | flops | bytes accessed | tf_op | source)
XLA Modules:
  0.0 24.4 jit_solution(13116923140122596903)
XLA Ops:
  1.3 22.1 %shard_map.146 = (bf16[64,8192]{1,0:T(8,128)(2,1)S(1)}, f32[8,128]{1,0:T(8,128)S(1)}, s32[8,128]{1,0:T(8,128)S(1)}, f32[8,128]{1,0:T(8,128)S(1)}, f32[1,128]{1,0:T(1,128)S(1)}) custom-call(bf16[64,256]{1,0:T(8,128)(2,1)} %ns_hbm.1, bf16[64,256]{1,0:T(8,128)(2,1)} %nm_hbm.1, bf16[64,8192]{1,0:T(8,128)(2,1)} %sec_hbm.1, bf16[64,8192]{1,0:T(8,128)(2,1)} %mst_hbm.1, ...), custom_call_target="tpu_custom_call" | custom-call | tf_op jit(solution)/shard_map/pallas_call | solution.py:398
  23.4 1.0 %shard_map.147 = (bf16[64,8192]{1,0:T(8,128)(2,1)}, f32[8,128]{1,0:T(8,128)}, s32[8,128]{1,0:T(8,128)}, f32[8,128]{1,0:T(8,128)}, f32[1,128]{1,0:T(1,128)}) custom-call(bf16[64,8192]{1,0:T(8,128)(2,1)S(1)} %get-tuple-element.15.refs_0_, f32[8,128]{1,0:T(8,128)S(1)} %get-tuple-element.16.refs_1_, s32[8,128]{1,0:T(8,128)S(1)} %get-tuple-element.17.refs_2_, ...), custom_call_target="tpu_custom_call" | custom-call | tf_op jit(solution)/shard_map/pallas_call | solution.py:447
